TPU v7x, 128 devices: a whole 4x4x4 slice. The times are simulated.
128 devices in a mesh: tp: 4 (over x), sp: 32 (over z, y, core).
Axes of the slice: x: 4, y: 4, z: 4, core: 2. Of those that a mesh axis runs over, the one named last changes fastest.
Arguments:
- x_tok: bfloat16 [256, 3584], replicated
- seq_lens: int32 [256], replicated
- k_cache: bfloat16 [256, 1024, 4, 128], P(None, 'sp', 'tp')
- v_cache: bfloat16 [256, 1024, 4, 128], P(None, 'sp', 'tp')
- g_attn: bfloat16 [3584], replicated
- w_q: bfloat16 [3584, 3584], P(None, 'tp')
- w_k: bfloat16 [3584, 512], P(None, 'tp')
- w_v: bfloat16 [3584, 512], P(None, 'tp')
- w_o: bfloat16 [3584, 3584], P('tp')
- g_mlp: bfloat16 [3584], replicated
- w_gate: bfloat16 [3584, 18944], P(None, 'tp')
- w_up: bfloat16 [3584, 18944], P(None, 'tp')
- w_down: bfloat16 [18944, 3584], P('tp')
Outputs:
- output 1: bfloat16 [256, 3584], replicated
- output 2: bfloat16 [256, 1024, 4, 128], P(None, 'sp', 'tp')
- output 3: bfloat16 [256, 1024, 4, 128], P(None, 'sp', 'tp')
All inputs are finite; a program needn't handle non-finite values.
Results may differ from a plain program's by a relative error of at most 0.0140962.
Values sent between devices are 32-bit elements.
A program may use at most 1 GiB of HBM per device.

v0:
```python
import jax
import jax.numpy as jnp
from jax import lax
from jax.sharding import PartitionSpec as P

ROPE_BASE = 500000.0
NORM_EPS = 1e-5


def rms_norm(x_in, norm_gain):
    x_f32 = x_in.astype(jnp.float32)
    inv_rms = lax.rsqrt(jnp.mean(x_f32 * x_f32, axis=-1, keepdims=True) + NORM_EPS)
    return (x_f32 * inv_rms * norm_gain.astype(jnp.float32)).astype(jnp.bfloat16)


def apply_rope(heads_in, positions):
    head_dim = heads_in.shape[-1]
    half_dim = head_dim // 2
    inv_freq = jnp.power(jnp.float32(ROPE_BASE), jnp.arange(half_dim, dtype=jnp.float32) * (-2.0 / head_dim))
    angles = positions.astype(jnp.float32)[:, None, None] * inv_freq
    cos_a = jnp.cos(angles)
    sin_a = jnp.sin(angles)
    heads_f32 = heads_in.astype(jnp.float32)
    first_half = heads_f32[..., :half_dim]
    second_half = heads_f32[..., half_dim:]
    rotated = jnp.concatenate([first_half * cos_a - second_half * sin_a, second_half * cos_a + first_half * sin_a], axis=-1)
    return rotated.astype(jnp.bfloat16)


def solution(mesh):
    cache_spec = P(None, "sp", "tp", None)
    col_spec = P(None, "tp")
    row_spec = P("tp", None)
    full_spec = P()

    def local_step(x_tok, seq_lens, k_blk, v_blk, g_attn, wq_loc, wk_loc, wv_loc, wo_loc, g_mlp, wg_loc, wu_loc, wd_loc):
        batch_rows, seq_blk, kv_loc, head_dim = k_blk.shape
        q_loc = wq_loc.shape[1] // head_dim
        groups = q_loc // kv_loc
        x_norm = rms_norm(x_tok, g_attn)
        q_new = jnp.dot(x_norm, wq_loc, preferred_element_type=jnp.float32).astype(jnp.bfloat16).reshape(batch_rows, q_loc, head_dim)
        k_new = jnp.dot(x_norm, wk_loc, preferred_element_type=jnp.float32).astype(jnp.bfloat16).reshape(batch_rows, kv_loc, head_dim)
        v_new = jnp.dot(x_norm, wv_loc, preferred_element_type=jnp.float32).astype(jnp.bfloat16).reshape(batch_rows, kv_loc, head_dim)
        q_rot = apply_rope(q_new, seq_lens)
        k_rot = apply_rope(k_new, seq_lens)
        local_pos = lax.axis_index("sp") * seq_blk + jnp.arange(seq_blk)
        is_new = (local_pos[None, :] == seq_lens[:, None])[:, :, None, None]
        k_out = jnp.where(is_new, k_rot[:, None], k_blk)
        v_out = jnp.where(is_new, v_new[:, None], v_blk)
        q_grp = q_rot.reshape(batch_rows, kv_loc, groups, head_dim)
        scores = jnp.einsum("bkgd,bskd->bkgs", q_grp, k_out, preferred_element_type=jnp.float32) * (head_dim ** -0.5)
        is_valid = (local_pos[None, :] <= seq_lens[:, None])[:, None, None, :]
        masked = jnp.where(is_valid, scores, -1e30)
        blk_max = jnp.max(masked, axis=-1, keepdims=True)
        weights = jnp.where(is_valid, jnp.exp(masked - blk_max), 0.0)
        blk_sum = jnp.sum(weights, axis=-1, keepdims=True)
        blk_mix = jnp.einsum("bkgs,bskd->bkgd", weights.astype(jnp.bfloat16), v_out, preferred_element_type=jnp.float32)
        glob_max = lax.pmax(blk_max, "sp")
        factor = jnp.exp(blk_max - glob_max)
        packed = lax.psum(jnp.concatenate([blk_mix * factor, blk_sum * factor], axis=-1), "sp")
        attn_out = (packed[..., :head_dim] / packed[..., head_dim:]).astype(jnp.bfloat16).reshape(batch_rows, q_loc * head_dim)
        attn_proj = lax.psum(jnp.dot(attn_out, wo_loc, preferred_element_type=jnp.float32), "tp")
        hidden = (x_tok.astype(jnp.float32) + attn_proj).astype(jnp.bfloat16)
        h_norm = rms_norm(hidden, g_mlp)
        gate_proj = jnp.dot(h_norm, wg_loc, preferred_element_type=jnp.float32).astype(jnp.bfloat16)
        up_proj = jnp.dot(h_norm, wu_loc, preferred_element_type=jnp.float32).astype(jnp.bfloat16)
        act_prod = (jax.nn.silu(gate_proj.astype(jnp.float32)) * up_proj.astype(jnp.float32)).astype(jnp.bfloat16)
        mlp_out = lax.psum(jnp.dot(act_prod, wd_loc, preferred_element_type=jnp.float32), "tp")
        y_out = (hidden.astype(jnp.float32) + mlp_out).astype(jnp.bfloat16)
        return y_out, k_out, v_out

    return jax.shard_map(local_step, mesh=mesh, in_specs=(full_spec, full_spec, cache_spec, cache_spec, full_spec, col_spec, col_spec, col_spec, row_spec, full_spec, col_spec, col_spec, row_spec), out_specs=(full_spec, cache_spec, cache_spec), check_vma=False)
```

profile of v0, /device:TPU:1, one launch (start us, length us, event | category | flops | bytes accessed | tf_op | source)
XLA Modules:
  0.0 459.7 jit_solution(14964792060258557431)
XLA Ops:
  7.3 0.8 convert_element_type.89
  8.1 2.1 fusion.10
  10.2 0.7 convert_element_type.84
  10.9 0.8 broadcast_compare_fusion.1
  11.7 2.8 convolution_convert_fusion.3
  14.6 0.9 fusion.37
  15.5 1.2 multiply_cosine_fusion
  17.0 0.7 copy.58
  17.8 5.9 %fusion.35 = f32[256,896]{1,0:T(8,128)} fusion(bf16[3584,896]{1,0:T(8,128)(2,1)} %param.18, bf16[256,3584]{1,0:T(8,128)(2,1)S(1)} %copy-done.3, f32[3584]{0:T(1024)S(1)} %convert_element_type.84, f32[256]{0:T(256)S(1)} %add_rsqrt_fusion.1), kind=kOutput, calls=%fused_computation.39 | convolution fusion | flops 1648295936 | bytes 9190400 | tf_op jit(solution)/shard_map/dot_general | solution.py:41
  23.7 1.5 copy.55
  25.2 0.4 copy.74
  25.7 0.4 copy.73
  26.1 1.4 subtract_convert_fusion
  27.8 5.5 %broadcast_select_fusion = (bf16[256,32,1,128]{3,1,2,0:T(8,128)(2,1)}, bf16[256,32,1,128]{3,1,2,0:T(8,128)(2,1)S(1)}) fusion(bf16[256,32,1,128]{3,1,2,0:T(8,128)(2,1)S(1)} %copy-done.5, pred[256,32]{1,0:T(8,128)(4,1)S(1)} %get-tuple-element.16, bf16[256,128]{1,0:T(8,128)(2,1)S(1)} %copy-done.7, bf16[256,32,1,128]{3,1,2,0:T(8,128)(2,1)} %param.15, ...), kind=kLoop, calls=%fused_computation.32 | loop fusion | flops 2097152 | bytes 8527872 | tf_op jit(solution)/shard_map/jit(_where)/select_n | solution.py:49
  33.3 2.2 fusion.70
  35.6 66.0 %pmax.7 = f32[256,1,7,1]{0,3,2,1:T(1,128)S(1)} all-reduce(f32[256,1,7,1]{0,3,2,1:T(1,128)S(1)} %copy.61), channel_id=1, replica_groups=mesh['tp'=4,'sp'=32] {'sp'}, use_global_device_ids=true, to_apply=%region_2.3 | all-reduce | flops 1792 | bytes 14336 | tf_op jit(solution)/shard_map/pmax | solution.py:58
  101.7 1.9 fusion.39
  103.8 1.3 copy.65
  105.2 2.7 fusion.32
  107.9 1.5 pad_maximum_fusion
  109.7 108.3 %all-reduce.4.cloned.1.call-done = f32[256,1,7,129]{3,2,0,1:T(8,128)} async-done(((f32[256,1,7,129]{3,2,0,1:T(8,128)}), f32[256,1,7,129]{3,2,0,1:T(8,128)}) %all-reduce.4.cloned.1.call-update) | async-done | bytes 924688 | tf_op jit(solution)/shard_map/psum | solution.py:60
  218.0 1.3 slice.29
  219.3 1.6 copy.72
  220.9 1.6 fusion.38
  222.8 6.8 %fusion.71 = f32[256,3584]{1,0:T(8,128)} fusion(bf16[256,896]{0,1:T(8,128)(2,1)S(1)} %bitcast.43, bf16[896,3584]{1,0:T(8,128)(2,1)} %param.21), kind=kOutput, calls=%fused_computation.85 | convolution fusion | flops 1644167168 | bytes 10551296 | tf_op jit(solution)/shard_map/dot_general | solution.py:62
  229.6 0.6 copy-done.8
  230.3 82.5 %all-reduce.6.cloned.1.call-done = f32[256,3584]{1,0:T(8,128)} async-done(((f32[256,3584]{1,0:T(8,128)}), f32[256,3584]{1,0:T(8,128)}) %all-reduce.6.cloned.1.call-update) | async-done | bytes 3670032 | tf_op jit(solution)/shard_map/psum | solution.py:62
  312.8 3.3 fusion.14
  316.1 17.7 %fusion.3 = f32[256,4736]{1,0:T(8,128)} fusion(bf16[3584,4736]{1,0:T(8,128)(2,1)} %param.23, bf16[256,3584]{1,0:T(8,128)(2,1)S(1)} %get-tuple-element.4, f32[3584]{0:T(1024)S(1)} %convert_element_type.98, f32[256]{0:T(256)S(1)} %add_rsqrt_fusion), kind=kOutput, calls=%fused_computation.5 | convolution fusion | flops 8696692736 | bytes 40647680 | tf_op jit(solution)/shard_map/dot_general | solution.py:65
  333.7 31.7 %fusion.4 = f32[256,3584]{1,0:T(8,128)} fusion(bf16[4736,3584]{1,0:T(8,128)(2,1)} %param.25, bf16[3584,4736]{1,0:T(8,128)(2,1)} %param.24, f32[256,4736]{1,0:T(8,128)} %fusion.3, bf16[256,3584]{1,0:T(8,128)(2,1)S(1)} %get-tuple-element.4, f32[3584]{0:T(1024)S(1)} %convert_element_type.98, f32[256]{0:T(256)S(1)} %add_rsqrt_fusion), kind=kOutput, calls=%fused_computation.12 | convolution fusion | flops 17394565120 | bytes 78265344 | tf_op jit(solution)/shard_map/dot_general | solution.py:68
  365.5 84.0 %all-reduce.8.cloned.1.call-done = f32[256,3584]{1,0:T(8,128)} async-done(((f32[256,3584]{1,0:T(8,128)}), f32[256,3584]{1,0:T(8,128)}) %all-reduce.8.cloned.1.call-update) | async-done | bytes 3670032 | tf_op jit(solution)/shard_map/psum | solution.py:68
  449.5 3.7 fusion.17
  (39 shorter events, 1.8 us)
Async XLA Ops:
  7.2 4.6 copy-start
  7.2 7.4 %copy-start.3 = (bf16[256,3584]{1,0:T(8,128)(2,1)S(1)}, bf16[256,3584]{1,0:T(8,128)(2,1)}, u32[]{:S(2)}) copy-start(bf16[256,3584]{1,0:T(8,128)(2,1)} %param.13) | copy-start | bytes 5505028
  7.2 210.8 %all-reduce.4.cloned.1.call-start = ((), (), s32[]{:S(2)}) async-start(), calls=%async_computation | async-start | bytes 4194304 | tf_op jit(solution)/shard_map/psum | solution.py:60
  7.3 7.3 %copy-start.9 = (bf16[3584,128]{1,0:T(8,128)(2,1)S(1)}, bf16[3584,128]{1,0:T(8,128)(2,1)}, u32[]{:S(2)}) copy-start(bf16[3584,128]{1,0:T(8,128)(2,1)} %param.19) | copy-start | bytes 2752516
  25.2 2.3 copy-start.6
  25.2 2.3 copy-start.7
  26.1 1.7 copy-start.5
  33.3 74.6 %copy-start.2 = (bf16[256,32,1,128]{3,1,2,0:T(8,128)(2,1)}, bf16[256,32,1,128]{3,1,2,0:T(8,128)(2,1)S(1)}, u32[]{:S(2)}) copy-start(bf16[256,32,1,128]{3,1,2,0:T(8,128)(2,1)S(1)} %get-tuple-element.14) | copy-start | bytes 6291460
  105.1 2.8 copy-start.4
  109.5 203.3 %all-reduce.6.cloned.1.call-start = ((), (), s32[]{:S(2)}) async-start(), calls=%async_computation.1 | async-start | bytes 7340032 | tf_op jit(solution)/shard_map/psum | solution.py:62
  229.6 0.7 copy-start.8
  229.6 219.9 %all-reduce.8.cloned.1.call-start = ((), (), s32[]{:S(2)}) async-start(), calls=%async_computation.2 | async-start | bytes 7340032 | tf_op jit(solution)/shard_map/psum | solution.py:68
  365.5 87.7 %copy-start.1 = (bf16[3584,128]{1,0:T(8,128)(2,1)S(1)}, bf16[3584,128]{1,0:T(8,128)(2,1)}, u32[]{:S(2)}) copy-start(bf16[3584,128]{1,0:T(8,128)(2,1)} %param.20) | copy-start | bytes 2752516
Sparse Core Ops, SparseCore 0:
  109.6 108.3 all-reduce.3
  229.7 83.0 all-reduce.5
  365.6 83.8 all-reduce.7
where the time goes:
time: 460 us
  waiting for transfers between devices  275 us (60%)
  matrix products  70.7 us (15%)
  blocking collectives  66 us (14%)
  other arithmetic  24.8 us (5%)
  between operations  14 us (3%)
  local copies, waits for them, and re-layouts  8.94 us (2%)
    psum x1, waiting for transfers between devices, local_step(): lax.psum(jnp.concatenate([blk_mix * factor, blk_sum * factor], axis=-1),...  108 us
    psum x1, waiting for transfers between devices, local_step(): lax.psum(jnp.dot(act_prod, wd_loc, preferred_element_type=jnp.float32), '...  84 us
    psum x1, waiting for transfers between devices, local_step(): lax.psum(jnp.dot(attn_out, wo_loc, preferred_element_type=jnp.float32), '...  82.5 us
    pmax x1, blocking collectives, local_step(): glob_max = lax.pmax(blk_max, 'sp')  66 us
    dot_general x1, matrix products, local_step(): jnp.dot(act_prod, wd_loc, preferred_element_type=jnp.float32)  31.7 us
    dot_general x1, matrix products, local_step(): jnp.dot(h_norm, wg_loc, preferred_element_type=jnp.float32)  17.7 us
  transfers between devices with their start and end apart: 3, of which 3 were waited for; matrix products, arithmetic and copies ran while one was open for 0% of the time, Pallas kernels for 0%

commit v1 on v0

v1 whole, which is shorter than its diff:
```python
import functools

import jax
import jax.numpy as jnp
from jax import lax
from jax.experimental import pallas as pl
from jax.experimental.pallas import tpu as pltpu
from jax.sharding import PartitionSpec as P

ROPE_BASE = 500000.0
NORM_EPS = 1e-5
MESH = pl.DeviceIdType.MESH
F32 = jnp.float32
BF16 = jnp.bfloat16
NX, NZ, NY, NC = 4, 4, 4, 2
LANE = 128


def rms_norm(x_in, norm_gain):
    x_f32 = x_in.astype(F32)
    inv_rms = lax.rsqrt(jnp.mean(x_f32 * x_f32, axis=-1, keepdims=True) + NORM_EPS)
    return (x_f32 * inv_rms * norm_gain.astype(F32)).astype(BF16)


def apply_rope(heads_in, positions):
    head_dim = heads_in.shape[-1]
    half_dim = head_dim // 2
    inv_freq = jnp.power(F32(ROPE_BASE), jnp.arange(half_dim, dtype=F32) * (-2.0 / head_dim))
    angles = positions.astype(F32)[:, None, None] * inv_freq
    cos_a = jnp.cos(angles)
    sin_a = jnp.sin(angles)
    heads_f32 = heads_in.astype(F32)
    first_half = heads_f32[..., :half_dim]
    second_half = heads_f32[..., half_dim:]
    rotated = jnp.concatenate([first_half * cos_a - second_half * sin_a, second_half * cos_a + first_half * sin_a], axis=-1)
    return rotated.astype(BF16)


def coords():
    s = lax.axis_index("sp")
    return lax.axis_index("tp"), s // (NY * NC), (s // NC) % NY, s % NC


def dev(x, z, y, c):
    return (x, (z * NY + y) * NC + c)


def turn(v, d, n):
    return lax.rem(v + d, n)


def entry_barrier(peers):
    barrier = pltpu.get_barrier_semaphore()
    for peer in peers:
        pl.semaphore_signal(barrier, inc=1, device_id=peer, device_id_type=MESH)
    pl.semaphore_wait(barrier, len(peers))


def remote(src, dst, send_sem, recv_sem, peer):
    return pltpu.make_async_remote_copy(
        src_ref=src, dst_ref=dst, send_sem=send_sem, recv_sem=recv_sem, device_id=peer, device_id_type=MESH
    )


def row_chunk(z, y, c):
    return (z * NC + c) * NY + y


def combine_kernel(in_ref, out_ref, slots, send_sem, recv_sem):
    x, z, y, c = coords()
    hops = [(dz, dy, dc) for dz in range(NZ) for dy in range(NY) for dc in range(NC)][1:]
    peers = [(turn(z, dz, NZ), turn(y, dy, NY), turn(c, dc, NC)) for dz, dy, dc in hops]
    entry_barrier([dev(x, *p) for p in peers])
    copies = []
    for k, p in enumerate(peers):
        rows = pl.ds(pl.multiple_of(row_chunk(*p) * 8, 8), 8)
        copies.append(remote(in_ref.at[rows, :], slots.at[k], send_sem.at[k], recv_sem.at[k], dev(x, *p)))
    for copy in copies:
        copy.start()
    heads = out_ref.shape[1] // LANE
    hd = heads * LANE
    mine = pl.ds(pl.multiple_of(row_chunk(z, y, c) * 8, 8), 8)
    top = in_ref[mine, hd:]
    for k, copy in enumerate(copies):
        copy.wait_recv()
    for k in range(len(copies)):
        top = jnp.maximum(top, slots[k, :, hd:])

    def add(stats, mix, acc, total):
        factor = jnp.exp(stats - top)
        total = total + pltpu.roll(factor, LANE // 2, 1) * stats
        parts = [acc[:, h * LANE:(h + 1) * LANE] + factor[:, h:h + 1] * mix[:, h * LANE:(h + 1) * LANE] for h in range(heads)]
        return jnp.concatenate(parts, axis=1), total

    acc, total = add(in_ref[mine, hd:], in_ref[mine, :hd], jnp.zeros((8, hd), F32), jnp.zeros((8, LANE), F32))

    def body(k, carry):
        return add(slots[k, :, hd:], slots[k, :, :hd], *carry)

    acc, total = lax.fori_loop(0, len(copies), body, (acc, total))
    half = LANE // 2
    out = [acc[:, h * LANE:(h + 1) * LANE] / total[:, half + h:half + h + 1] for h in range(heads)]
    out_ref[...] = jnp.concatenate(out, axis=1).astype(out_ref.dtype)
    for copy in copies:
        copy.wait_send()


def combine(packed, heads):
    width = packed.shape[1]
    return pl.pallas_call(
        combine_kernel,
        name="combine",
        out_shape=jax.ShapeDtypeStruct((8, heads * LANE), BF16),
        in_specs=[pl.BlockSpec(memory_space=pltpu.VMEM)],
        out_specs=pl.BlockSpec(memory_space=pltpu.VMEM),
        scratch_shapes=[
            pltpu.VMEM((31, 8, width), F32),
            pltpu.SemaphoreType.DMA((31,)),
            pltpu.SemaphoreType.DMA((31,)),
        ],
        compiler_params=pltpu.CompilerParams(collective_id=0, has_side_effects=True),
    )(packed)


XY = [(dx, dy) for dx in range(NX) for dy in range(NY)][1:]


def hidden_kernel(part_ref, res_ref, hid_ref, slots, chunk, rs_send, rs_recv, ag_send, ag_recv):
    x, z, y, c = coords()
    w = chunk.shape[1]
    plane = [(turn(x, dx, NX), turn(y, dy, NY)) for dx, dy in XY]
    entry_barrier([dev(px, z, py, c) for px, py in plane])
    rs = []
    for k in range(1, NX):
        px = turn(x, k, NX)
        cols = pl.ds(pl.multiple_of(px * w, LANE), w)
        rs.append(remote(part_ref.at[:, cols], slots.at[k - 1], rs_send.at[k - 1], rs_recv.at[k - 1], dev(px, z, y, c)))
    for copy in rs:
        copy.start()
    my_cols = pl.ds(pl.multiple_of(x * w, LANE), w)
    my_rows = pl.ds(pl.multiple_of(y * 8, 8), 8)
    total = part_ref[:, my_cols]
    for k, copy in enumerate(rs):
        copy.wait_recv()
        total = total + slots[k]
    hidden = (res_ref[...] + total).astype(BF16).astype(F32)
    chunk[...] = hidden
    ag = []
    for k, (px, py) in enumerate(plane):
        ag.append(remote(chunk, hid_ref.at[my_rows, my_cols], ag_send.at[k], ag_recv.at[k], dev(px, z, py, c)))
    for copy in ag:
        copy.start()
    hid_ref[my_rows, my_cols] = hidden
    for copy in ag:
        copy.wait_recv()
    for copy in rs + ag:
        copy.wait_send()


def gather_hidden(part, res):
    width = part.shape[1]
    w = width // NX
    return pl.pallas_call(
        hidden_kernel,
        name="gather_hidden",
        out_shape=jax.ShapeDtypeStruct((8 * NY, width), F32),
        in_specs=[pl.BlockSpec(memory_space=pltpu.VMEM)] * 2,
        out_specs=pl.BlockSpec(memory_space=pltpu.VMEM),
        scratch_shapes=[
            pltpu.VMEM((NX - 1, 8, w), F32),
            pltpu.VMEM((8, w), F32),
            pltpu.SemaphoreType.DMA((NX - 1,)),
            pltpu.SemaphoreType.DMA((NX - 1,)),
            pltpu.SemaphoreType.DMA((15,)),
            pltpu.SemaphoreType.DMA((15,)),
        ],
        compiler_params=pltpu.CompilerParams(collective_id=1, has_side_effects=True),
    )(part, res)


WIN = 256


def mlp_kernel(hid_ref, g_ref, wg_hbm, wu_hbm, wd_hbm, out_ref, wg, wu, wd, hn, sem):
    _, _, y, _ = coords()
    steps = wg.shape[0]
    ff_tiles = wg_hbm.shape[1] // LANE
    win_tiles = steps * WIN // LANE
    lo = (y * ff_tiles + NY - 1) // NY
    hi = ((y + 1) * ff_tiles + NY - 1) // NY
    first = jnp.minimum(lo, ff_tiles - win_tiles)
    base = first * LANE

    def fetch(i):
        cols = pl.ds(pl.multiple_of(base + i * WIN, LANE), WIN)
        return (
            pltpu.make_async_copy(wg_hbm.at[:, cols], wg.at[i], sem.at[0, i]),
            pltpu.make_async_copy(wu_hbm.at[:, cols], wu.at[i], sem.at[1, i]),
            pltpu.make_async_copy(wd_hbm.at[cols, :], wd.at[i], sem.at[2, i]),
        )

    for i in range(steps):
        for copy in fetch(i):
            copy.start()
    hid = hid_ref[...]
    inv = lax.rsqrt(jnp.mean(hid * hid, axis=-1, keepdims=True) + NORM_EPS)
    hn[...] = (hid * inv * g_ref[...].astype(F32)).astype(BF16)
    out_ref[...] = jnp.zeros_like(out_ref)

    def body(i, carry):
        cg, cu, cd = fetch(i)
        cg.wait()
        gate = jnp.dot(hn[...], wg[i], preferred_element_type=F32).astype(BF16).astype(F32)
        cu.wait()
        up = jnp.dot(hn[...], wu[i], preferred_element_type=F32).astype(BF16).astype(F32)
        act = jax.nn.silu(gate) * up
        col = lax.broadcasted_iota(jnp.int32, act.shape, 1) + (base + i * WIN)
        act = jnp.where((col >= lo * LANE) & (col < hi * LANE), act, 0.0).astype(BF16)
        cd.wait()
        out_ref[...] += jnp.dot(act, wd[i], preferred_element_type=F32)
        return carry

    lax.fori_loop(0, steps, body, 0)


def mlp(hid, g, wg, wu, wd):
    rows, width = hid.shape
    ff_tiles = wg.shape[1] // LANE
    steps = -(-(-(-ff_tiles // NY)) * LANE // WIN)
    return pl.pallas_call(
        mlp_kernel,
        name="mlp",
        out_shape=jax.ShapeDtypeStruct((rows, width), F32),
        in_specs=[pl.BlockSpec(memory_space=pltpu.VMEM)] * 2 + [pl.BlockSpec(memory_space=pl.ANY)] * 3,
        out_specs=pl.BlockSpec(memory_space=pltpu.VMEM),
        scratch_shapes=[
            pltpu.VMEM((steps, width, WIN), BF16),
            pltpu.VMEM((steps, width, WIN), BF16),
            pltpu.VMEM((steps, WIN, width), BF16),
            pltpu.VMEM((rows, width), BF16),
            pltpu.SemaphoreType.DMA((3, steps)),
        ],
        compiler_params=pltpu.CompilerParams(vmem_limit_bytes=48 * 2**20),
        cost_estimate=pl.CostEstimate(flops=6 * rows * width * steps * WIN, bytes_accessed=6 * width * steps * WIN, transcendentals=0),
    )(hid, g.reshape(1, -1), wg, wu, wd)


def output_kernel(part_ref, hid_ref, buf, slots, chunk, rs_send, rs_recv, p1_send, p1_recv, p2_send, p2_recv, cc_send, cc_recv):
    x, z, y, c = coords()
    w = chunk.shape[1]
    cut = [(0, 256), (256, 256), (512, w - 512)]
    plane = [(turn(x, dx, NX), turn(y, dy, NY)) for dx, dy in XY]
    first = [
        [(turn(x, a, NX), z, turn(y, b, NY)) for a, b in XY],
        [(x, turn(z, a, NZ), turn(y, b, NY)) for a, b in XY],
        [(turn(x, a, NX), turn(z, b, NZ), y) for a, b in XY],
    ]
    second = [
        [(x, turn(z, k, NZ), y) for k in range(1, 4)],
        [(turn(x, k, NX), z, y) for k in range(1, 4)],
        [(x, z, turn(y, k, NY)) for k in range(1, 4)],
    ]
    partner = dev(x, z, y, turn(c, 1, NC))
    near = [(turn(x, a, NX), z, turn(y, b, NY)) for a, b in XY]
    near += [(x, turn(z, a, NZ), turn(y, b, NY)) for a in range(1, NZ) for b in range(NY)]
    near += [(turn(x, a, NX), turn(z, b, NZ), y) for a in range(1, NX) for b in range(1, NZ)]
    entry_barrier([dev(*p, c) for p in near] + [partner])
    rs = []
    for k, (px, py) in enumerate(plane):
        rows = pl.ds(pl.multiple_of(py * 8, 8), 8)
        cols = pl.ds(pl.multiple_of(px * w, LANE), w)
        rs.append(remote(part_ref.at[rows, cols], slots.at[k], rs_send.at[k], rs_recv.at[k], dev(px, z, py, c)))
    for copy in rs:
        copy.start()
    my_rows = pl.ds(pl.multiple_of(y * 8, 8), 8)
    my_cols = pl.ds(pl.multiple_of(x * w, LANE), w)
    total = part_ref[my_rows, my_cols]
    for k, copy in enumerate(rs):
        copy.wait_recv()
        total = total + slots[k]
    out = (hid_ref[my_rows, my_cols] + total).astype(BF16).astype(F32)
    chunk[...] = out
    p1 = []
    for part, (lo, n) in enumerate(cut):
        for k, p in enumerate(first[part]):
            src = chunk.at[:, lo:lo + n]
            dst = buf.at[z, c, y, x, :, lo:lo + n]
            p1.append(remote(src, dst, p1_send.at[part, k], p1_recv.at[part, k], dev(*p, c)))
    for copy in p1:
        copy.start()
    buf[z, c, y, x] = out
    p2 = []
    for part, (lo, n) in enumerate(cut):
        for copy in p1[part * 15:(part + 1) * 15]:
            copy.wait_recv()
        block = [
            buf.at[z, c, :, :, :, lo:lo + n],
            buf.at[:, c, :, x, :, lo:lo + n],
            buf.at[:, c, y, :, :, lo:lo + n],
        ][part]
        for k, p in enumerate(second[part]):
            copy = remote(block, block, p2_send.at[part, k], p2_recv.at[part, k], dev(*p, c))
            copy.start()
            p2.append(copy)
    for copy in p2:
        copy.wait_recv()
    across = remote(buf.at[:, c], buf.at[:, c], cc_send, cc_recv, partner)
    across.start()
    across.wait_recv()
    for copy in rs + p1 + p2 + [across]:
        copy.wait_send()


def gather_output(part, hid):
    width = part.shape[1]
    w = width // NX
    sem = pltpu.SemaphoreType.DMA
    return pl.pallas_call(
        output_kernel,
        name="gather_output",
        out_shape=jax.ShapeDtypeStruct((NZ, NC, NY, NX, 8, w), F32),
        in_specs=[pl.BlockSpec(memory_space=pltpu.VMEM)] * 2,
        out_specs=pl.BlockSpec(memory_space=pltpu.VMEM),
        scratch_shapes=[
            pltpu.VMEM((15, 8, w), F32),
            pltpu.VMEM((8, w), F32),
            sem((15,)), sem((15,)), sem((3, 15)), sem((3, 15)), sem((3, 3)), sem((3, 3)), sem, sem,
        ],
        compiler_params=pltpu.CompilerParams(collective_id=2, has_side_effects=True),
    )(part, hid)


def solution(mesh):
    cache_spec = P(None, "sp", "tp", None)
    col_spec = P(None, "tp")
    row_spec = P("tp", None)
    full_spec = P()

    def local_step(x_tok, seq_lens, k_blk, v_blk, g_attn, wq_loc, wk_loc, wv_loc, wo_loc, g_mlp, wg_loc, wu_loc, wd_loc):
        batch_rows, seq_blk, kv_loc, head_dim = k_blk.shape
        q_loc = wq_loc.shape[1] // head_dim
        groups = q_loc // kv_loc
        x, z, y, c = coords()
        w = x_tok.shape[1] // NX
        res = lax.dynamic_slice(x_tok, (row_chunk(z, y, c) * 8, x * w), (8, w)).astype(F32)
        x_norm = rms_norm(x_tok, g_attn)
        q_new = jnp.dot(x_norm, wq_loc, preferred_element_type=F32).astype(BF16).reshape(batch_rows, q_loc, head_dim)
        k_new = jnp.dot(x_norm, wk_loc, preferred_element_type=F32).astype(BF16).reshape(batch_rows, kv_loc, head_dim)
        v_new = jnp.dot(x_norm, wv_loc, preferred_element_type=F32).astype(BF16).reshape(batch_rows, kv_loc, head_dim)
        q_rot = apply_rope(q_new, seq_lens)
        k_rot = apply_rope(k_new, seq_lens)
        local_pos = lax.axis_index("sp") * seq_blk + jnp.arange(seq_blk)
        is_new = (local_pos[None, :] == seq_lens[:, None])[:, :, None, None]
        k_out = jnp.where(is_new, k_rot[:, None], k_blk)
        v_out = jnp.where(is_new, v_new[:, None], v_blk)
        q_grp = q_rot.reshape(batch_rows, kv_loc, groups, head_dim)
        scores = jnp.einsum("bkgd,bskd->bkgs", q_grp, k_out, preferred_element_type=F32) * (head_dim ** -0.5)
        is_valid = (local_pos[None, :] <= seq_lens[:, None])[:, None, None, :]
        masked = jnp.where(is_valid, scores, -1e30)
        blk_max = jnp.max(masked, axis=-1, keepdims=True)
        weights = jnp.where(is_valid, jnp.exp(masked - blk_max), 0.0)
        blk_sum = jnp.sum(weights, axis=-1, keepdims=True)
        blk_mix = jnp.einsum("bkgs,bskd->bkgd", weights.astype(BF16), v_out, preferred_element_type=F32)
        half = LANE // 2
        pad = jnp.zeros((batch_rows, half - q_loc), F32)
        packed = jnp.concatenate(
            [blk_mix.reshape(batch_rows, q_loc * head_dim), blk_max.reshape(batch_rows, q_loc), pad, blk_sum.reshape(batch_rows, q_loc), pad], axis=1
        )
        attn_out = combine(packed, q_loc)
        part = jnp.dot(attn_out, wo_loc, preferred_element_type=F32)
        hid = gather_hidden(part, res)
        mlp_part = mlp(hid, g_mlp, wg_loc, wu_loc, wd_loc)
        buf = gather_output(mlp_part, hid)
        y_out = buf.transpose(0, 1, 2, 4, 3, 5).reshape(x_tok.shape).astype(BF16)
        return y_out, k_out, v_out

    return jax.shard_map(local_step, mesh=mesh, in_specs=(full_spec, full_spec, cache_spec, cache_spec, full_spec, col_spec, col_spec, col_spec, row_spec, full_spec, col_spec, col_spec, row_spec), out_specs=(full_spec, cache_spec, cache_spec), check_vma=False)
```

time: 460 us -> 137 us (0.30)
  waiting for transfers between devices: 275 us -> 0 us
  Pallas kernels: 0 us -> 95.6 us
  blocking collectives: 66 us -> 0 us
  matrix products: 70.7 us -> 14.6 us
  between operations: 14 us -> 0.96 us
  other arithmetic: 24.8 us -> 15.9 us
    psum x3 -> x0, waiting for transfers between devices: 275 us -> none  [the longest x1 108 us: local_step(): lax.psum(jnp.concatenate([blk_mix * factor, blk_sum * factor], axis=-1),...]
    pallas_call x0 -> x4, Pallas kernels: none -> 95.6 us  [the longest x1 41.8 us: gather_output(): pl.pallas_call(output_kernel, name='gather_output', out_shape=jax.ShapeDt...]
    pmax x1 -> x0, blocking collectives: 66 us -> none  [local_step(): glob_max = lax.pmax(blk_max, 'sp')]
    dot_general x8 -> x6, matrix products: 70.7 us -> 14.6 us  [the longest x1 5.87 us: local_step(): jnp.dot(x_norm, wq_loc, preferred_element_type=F32).astype(BF16)]
  transfers between devices with their start and end apart: 3 -> 0, of which waited for: 3 -> 0; matrix products, arithmetic and copies ran while one was open for 0% -> 0% of each run, Pallas kernels for 0% -> 0%
where the time goes in v1:
time: 137 us; the launch traced here: 136 us
  Pallas kernels  95.6 us (70%)
  other arithmetic  15.9 us (12%)
  matrix products  14.6 us (11%)
  local copies, waits for them, and re-layouts  8.92 us (7%)
    pallas_call x1, Pallas kernels, gather_output(): pl.pallas_call(output_kernel, name='gather_output', out_shape=jax.ShapeDt...  41.8 us
    pallas_call x1, Pallas kernels, combine(): pl.pallas_call(combine_kernel, name='combine', out_shape=jax.ShapeDtypeSt...  28.8 us
    pallas_call x1, Pallas kernels, gather_hidden(): pl.pallas_call(hidden_kernel, name='gather_hidden', out_shape=jax.ShapeDt...  15.2 us
    pallas_call x1, Pallas kernels, mlp(): pl.pallas_call(mlp_kernel, name='mlp', out_shape=jax.ShapeDtypeStruct((ro...  9.84 us
    dot_general x1, matrix products, local_step(): jnp.dot(x_norm, wq_loc, preferred_element_type=F32).astype(BF16)  5.87 us
    dot_general x1, matrix products, local_step(): part = jnp.dot(attn_out, wo_loc, preferred_element_type=F32)  4.43 us
    select_n x1, other arithmetic, local_step(): k_out = jnp.where(is_new, k_rot[:, None], k_blk)  4.21 us
    unnamed x28, local copies, waits for them, and re-layouts  4.07 us

profile of v1, /device:TPU:1, one launch (start us, length us, event | category | flops | bytes accessed | tf_op | source)
XLA Modules:
  0.0 136.0 jit_solution(13807622893063253513)
XLA Ops:
  0.7 0.8 convert_element_type.66
  1.6 1.9 %fusion = f32[256]{0:T(256)S(1)} fusion(bf16[256,3584]{1,0:T(8,128)(2,1)} %param.13), kind=kLoop, calls=%fused_computation.2 | loop fusion | flops 2752256 | bytes 1836032 | tf_op jit(solution)/shard_map/reduce_sum | solution.py:21
  3.5 0.7 reshape.258.g_ref
  4.2 0.7 convert_element_type.61
  4.9 1.3 dynamic-slice_convert_fusion.res_ref
  6.3 0.8 broadcast_compare_fusion.1
  7.1 1.3 convolution_convert_fusion.1
  8.4 0.9 fusion.15
  9.3 0.3 fusion.34
  9.7 0.7 copy.20
  10.4 1.2 multiply_cosine_fusion
  11.6 5.9 %fusion.13 = f32[256,896]{1,0:T(8,128)} fusion(bf16[3584,896]{1,0:T(8,128)(2,1)} %param.18, bf16[256,3584]{1,0:T(8,128)(2,1)S(1)} %copy-done.7, f32[3584]{0:T(1024)S(1)} %convert_element_type.61, f32[256]{0:T(256)S(1)} %add_rsqrt_fusion), kind=kOutput, calls=%fused_computation.14 | convolution fusion | flops 1648295936 | bytes 9190400 | tf_op jit(solution)/shard_map/dot_general | solution.py:347
  17.5 1.5 %copy.17 = f32[256,896]{0,1:T(8,128)S(1)} copy(f32[256,896]{1,0:T(8,128)} %fusion.13) | data formatting | bytes 1835008 | tf_op jit(solution)/shard_map/convert_element_type | solution.py:32
  19.1 0.4 copy.24
  19.5 0.4 copy.23
  20.0 0.3 subtract_convert_fusion
  20.4 1.2 copy-done.6
  21.6 4.2 %broadcast_select_fusion.1 = (bf16[256,32,1,128]{3,1,2,0:T(8,128)(2,1)S(1)}, bf16[256,32,1,128]{3,1,2,0:T(8,128)(2,1)S(1)}) fusion(bf16[256,32,1,128]{3,1,2,0:T(8,128)(2,1)S(1)} %copy-done.6, pred[256,32]{1,0:T(8,128)(4,1)S(1)} %get-tuple-element.12, bf16[256,128]{1,0:T(8,128)(2,1)S(1)} %copy-done.10, bf16[256,32,1,128]{3,1,2,0:T(8,128)(2,1)} %param.16, ...), kind=kLoop, calls=%fused_computation.10 | loop fusion | flops 2097152 | bytes 8527872 | tf_op jit(solution)/shard_map/jit(_where)/select_n | solution.py:354
  25.9 1.3 fusion.41
  27.2 0.8 fusion.16
  28.0 0.7 fusion.3
  28.7 0.4 copy.21
  29.1 0.3 copy.22
  29.4 1.2 concatenate.27.in_ref
  30.6 28.8 %combine.1 = bf16[8,896]{1,0:T(8,128)(2,1)} custom-call(f32[256,1024]{1,0:T(8,128)} %concatenate.27.in_ref), custom_call_target="tpu_custom_call" | custom-call | tf_op jit(solution)/shard_map/combine/pallas_call | solution.py:110
  59.5 4.4 %fusion.42.part_ref = f32[8,3584]{1,0:T(8,128)} fusion(bf16[8,896]{1,0:T(8,128)(2,1)} %combine.1, bf16[896,3584]{1,0:T(8,128)(2,1)} %param.21), kind=kOutput, calls=%fused_computation.55 | convolution fusion | flops 51380224 | bytes 6551552 | tf_op jit(solution)/shard_map/dot_general | solution.py:370
  63.9 15.2 %gather_hidden.1.hid_ref = f32[32,3584]{1,0:T(8,128)} custom-call(f32[8,3584]{1,0:T(8,128)} %fusion.42.part_ref, f32[8,896]{1,0:T(8,128)} %dynamic-slice_convert_fusion.res_ref), custom_call_target="tpu_custom_call" | custom-call | tf_op jit(solution)/shard_map/gather_hidden/pallas_call | solution.py:163
  79.1 1.0 copy-done.2
  80.1 9.8 %mlp.1.part_ref = f32[32,3584]{1,0:T(8,128)S(1)} custom-call(f32[32,3584]{1,0:T(8,128)S(1)} %copy-done.2, bf16[1,3584]{1,0:T(2,128)(2,1)S(1)} %reshape.258.g_ref, bf16[3584,4736]{1,0:T(8,128)(2,1)} %wg_hbm.1, bf16[3584,4736]{1,0:T(8,128)(2,1)} %wu_hbm.1, bf16[4736,3584]{1,0:T(8,128)(2,1)} %wd_hbm.1), custom_call_target="tpu_custom_call" | custom-call | flops 880803840 | bytes 27525120 | tf_op jit(solution)/shard_map/mlp/pallas_call | solution.py:230
  89.9 0.8 copy-done.3
  90.7 41.8 %gather_output.1 = f32[4,2,4,4,8,896]{5,4,3,2,1,0:T(8,128)} custom-call(f32[32,3584]{1,0:T(8,128)} %copy-done.3, f32[32,3584]{1,0:T(8,128)} %gather_hidden.1.hid_ref), custom_call_target="tpu_custom_call" | custom-call | tf_op jit(solution)/shard_map/gather_output/pallas_call | solution.py:318
  132.5 3.5 %convert_element_type.73 = bf16[4,2,4,4,8,896]{5,4,3,2,1,0:T(8,128)(2,1)} convert(f32[4,2,4,4,8,896]{5,4,3,2,1,0:T(8,128)} %gather_output.1) | non-fusion elementwise | flops 917504 | bytes 5505024 | tf_op jit(solution)/shard_map/convert_element_type | solution.py:374
  (29 shorter events, 0.3 us)
Async XLA Ops:
  0.6 6.4 %copy-start = (bf16[3584,128]{1,0:T(8,128)(2,1)S(1)}, bf16[3584,128]{1,0:T(8,128)(2,1)}, u32[]{:S(2)}) copy-start(bf16[3584,128]{1,0:T(8,128)(2,1)} %param.20) | copy-start | bytes 2752516
  0.6 6.4 %copy-start.7 = (bf16[256,3584]{1,0:T(8,128)(2,1)S(1)}, bf16[256,3584]{1,0:T(8,128)(2,1)}, u32[]{:S(2)}) copy-start(bf16[256,3584]{1,0:T(8,128)(2,1)} %param.13) | copy-start | bytes 5505028
  7.1 1.4 %copy-start.12 = (bf16[3584,128]{1,0:T(8,128)(2,1)S(1)}, bf16[3584,128]{1,0:T(8,128)(2,1)}, u32[]{:S(2)}) copy-start(bf16[3584,128]{1,0:T(8,128)(2,1)} %param.19) | copy-start | bytes 2752516
  19.0 0.9 copy-start.8
  19.0 1.0 copy-start.9
  19.5 0.9 copy-start.10
  19.5 0.9 copy-start.11
  20.0 1.6 %copy-start.6 = (bf16[256,32,1,128]{3,1,2,0:T(8,128)(2,1)S(1)}, bf16[256,32,1,128]{3,1,2,0:T(8,128)(2,1)}, u32[]{:S(2)}) copy-start(bf16[256,32,1,128]{3,1,2,0:T(8,128)(2,1)} %param.15) | copy-start | bytes 6291460
  25.8 1.4 %copy-start.4 = (bf16[256,32,1,128]{3,1,2,0:T(8,128)(2,1)}, bf16[256,32,1,128]{3,1,2,0:T(8,128)(2,1)S(1)}, u32[]{:S(2)}) copy-start(bf16[256,32,1,128]{3,1,2,0:T(8,128)(2,1)S(1)} %get-tuple-element.9) | copy-start | bytes 6291460
  25.8 2.1 %copy-start.5 = (bf16[256,32,1,128]{3,1,2,0:T(8,128)(2,1)}, bf16[256,32,1,128]{3,1,2,0:T(8,128)(2,1)S(1)}, u32[]{:S(2)}) copy-start(bf16[256,32,1,128]{3,1,2,0:T(8,128)(2,1)S(1)} %get-tuple-element.10) | copy-start | bytes 6291460
  79.0 1.0 copy-start.2
  89.9 0.8 copy-start.3
  90.7 45.3 %copy-start.1 = (bf16[3584,128]{1,0:T(8,128)(2,1)S(1)}, bf16[3584,128]{1,0:T(8,128)(2,1)}, u32[]{:S(2)}) copy-start(bf16[3584,128]{1,0:T(8,128)(2,1)} %param.20) | copy-start | bytes 2752516

commit v2 on v1

--- a/solution.py
+++ b/solution.py
@@ -14,26 +14,6 @@
 BF16 = jnp.bfloat16
 NX, NZ, NY, NC = 4, 4, 4, 2
 LANE = 128
-
-
-def rms_norm(x_in, norm_gain):
-    x_f32 = x_in.astype(F32)
-    inv_rms = lax.rsqrt(jnp.mean(x_f32 * x_f32, axis=-1, keepdims=True) + NORM_EPS)
-    return (x_f32 * inv_rms * norm_gain.astype(F32)).astype(BF16)
-
-
-def apply_rope(heads_in, positions):
-    head_dim = heads_in.shape[-1]
-    half_dim = head_dim // 2
-    inv_freq = jnp.power(F32(ROPE_BASE), jnp.arange(half_dim, dtype=F32) * (-2.0 / head_dim))
-    angles = positions.astype(F32)[:, None, None] * inv_freq
-    cos_a = jnp.cos(angles)
-    sin_a = jnp.sin(angles)
-    heads_f32 = heads_in.astype(F32)
-    first_half = heads_f32[..., :half_dim]
-    second_half = heads_f32[..., half_dim:]
-    rotated = jnp.concatenate([first_half * cos_a - second_half * sin_a, second_half * cos_a + first_half * sin_a], axis=-1)
-    return rotated.astype(BF16)
 
 
 def coords():
@@ -330,6 +310,155 @@
     )(part, hid)
 
 
+GRP = 16
+SUB = 2
+
+
+def attend_kernel(lens_ref, lens_row, x_ref, g_ref, freq_ref, k_ref, v_ref, wq_hbm, wk_hbm, wv_hbm, pack_ref, ko_ref, vo_ref, w, q, knew, vnew, pos, sem):
+    step = pl.program_id(0)
+    rows = x_ref.shape[0]
+    heads = wq_hbm.shape[1] // LANE
+    seq = k_ref.shape[1]
+    half = LANE // 2
+    hd = heads * LANE
+    base = lax.axis_index("sp") * seq
+
+    @pl.when(step == 0)
+    def project():
+        odd = hd % (2 * LANE)
+        cuts = [(i, 2 * LANE) for i in range(0, hd - odd, 2 * LANE)]
+        copies = [[pltpu.make_async_copy(wq_hbm.at[:, a:a + n], w.at[:, a:a + n], sem.at[i])] for i, (a, n) in enumerate(cuts)]
+        n = len(cuts)
+        last = [
+            pltpu.make_async_copy(wq_hbm.at[:, hd - odd:], w.at[:, hd - odd:hd], sem.at[n]),
+            pltpu.make_async_copy(wk_hbm, w.at[:, hd:hd + LANE], sem.at[n + 1]),
+        ]
+        copies += [last, [pltpu.make_async_copy(wv_hbm, w.at[:, hd + LANE:], sem.at[n + 2])]]
+        cuts += [(hd - odd, odd + LANE), (hd + LANE, LANE)]
+        for group in copies:
+            for copy in group:
+                copy.start()
+        x32 = x_ref[...].astype(F32)
+        inv = lax.rsqrt(jnp.mean(x32 * x32, axis=-1, keepdims=True) + NORM_EPS)
+        u = (x32 * inv * g_ref[...].astype(F32)).astype(BF16)
+        eye = lax.broadcasted_iota(jnp.int32, (LANE, LANE), 0) == lax.broadcasted_iota(jnp.int32, (LANE, LANE), 1)
+        cols = []
+        for i in range(rows // LANE):
+            line = lens_row[i:i + 1, :].astype(F32)
+            col = jnp.sum(jnp.where(eye, line, 0.0), axis=1, keepdims=True)
+            pos[i * LANE:(i + 1) * LANE, :] = jnp.broadcast_to(col, (LANE, LANE)).astype(jnp.int32)
+            cols.append(col)
+        low = lax.broadcasted_iota(jnp.int32, (LANE, LANE), 1) < half
+        angles = jnp.where(low, cols[0], cols[1]) * freq_ref[...]
+        cos = jnp.cos(angles)
+        sin = jnp.sin(angles)
+        cos_r = pltpu.roll(cos, half, 1)
+        sin_r = pltpu.roll(sin, half, 1)
+        cos_t = jnp.concatenate([jnp.where(low, cos, cos_r), jnp.where(low, cos_r, cos)], axis=0)
+        sin_t = jnp.concatenate([jnp.where(low, -sin, sin_r), jnp.where(low, -sin_r, sin)], axis=0)
+        for group, (a, n) in zip(copies, cuts):
+            for copy in group:
+                copy.wait()
+            out = jnp.dot(u, w[:, a:a + n], preferred_element_type=F32).astype(BF16).astype(F32)
+            for j in range(0, n, LANE):
+                h = (a + j) // LANE
+                part = out[:, j:j + LANE]
+                if h <= heads:
+                    part = (part * cos_t + pltpu.roll(part, half, 1) * sin_t).astype(BF16)
+                if h < heads:
+                    q[h] = part
+                elif h == heads:
+                    knew[...] = part.astype(F32)
+                else:
+                    vnew[...] = part
+
+    ko_ref[...] = k_ref[...]
+    vo_ref[...] = v_ref[...]
+    first = step * SUB * GRP
+    line = lax.broadcasted_iota(jnp.int32, (seq, LANE), 0)
+
+    def put(b, carry):
+        at = lens_ref[first + b] - base
+
+        @pl.when((at >= 0) & (at < seq))
+        def _():
+            here = line == at
+            k_row = knew[pl.ds(first + b, 1), :]
+            v_row = vnew[pl.ds(first + b, 1), :]
+            ko_ref[b] = jnp.where(here, k_row, ko_ref[b].astype(F32)).astype(BF16)
+            vo_ref[b] = jnp.where(here, v_row, vo_ref[b].astype(F32)).astype(BF16)
+
+        return carry
+
+    lax.fori_loop(0, SUB * GRP, put, 0)
+    span = GRP * seq
+    col = lax.broadcasted_iota(jnp.int32, (GRP, span), 1)
+    own = (col // seq) == lax.broadcasted_iota(jnp.int32, (GRP, span), 0)
+    where_at = base + col % seq
+    lane = lax.broadcasted_iota(jnp.int32, (GRP, LANE), 1)
+    for s in range(SUB):
+        at = pl.ds(pl.multiple_of(first + s * GRP, GRP), GRP)
+        block = slice(s * GRP, (s + 1) * GRP)
+        qs = jnp.concatenate([q[h, at, :] for h in range(heads)], axis=0)
+        ks = ko_ref[block].reshape(span, LANE)
+        vs = vo_ref[block].reshape(span, LANE)
+        p = jnp.concatenate([pos[at, :]] * (span // LANE), axis=1)
+        valid = own & (where_at <= p)
+        valid = jnp.concatenate([valid.astype(F32)] * heads, axis=0) > 0.5
+        scores = lax.dot_general(qs, ks, (((1,), (1,)), ((), ())), preferred_element_type=F32) * (LANE ** -0.5)
+        scores = jnp.where(valid, scores, -1e30)
+        top = jnp.max(scores, axis=1, keepdims=True)
+        wt = jnp.where(valid, jnp.exp(scores - top), 0.0)
+        tot = jnp.sum(wt, axis=1, keepdims=True)
+        mix = jnp.dot(wt.astype(BF16), vs, preferred_element_type=F32)
+        stats = jnp.zeros((GRP, LANE), F32)
+        for h in range(heads):
+            part = slice(h * GRP, (h + 1) * GRP)
+            pack_ref[block, h * LANE:(h + 1) * LANE] = mix[part]
+            stats = jnp.where(lane == h, top[part], stats)
+            stats = jnp.where(lane == half + h, tot[part], stats)
+        pack_ref[block, hd:] = stats
+
+
+def attend(x_tok, seq_lens, k_blk, v_blk, g, wq, wk, wv):
+    rows, width = x_tok.shape
+    seq = k_blk.shape[1]
+    hd = wq.shape[1]
+    half = LANE // 2
+    freq = jnp.power(F32(ROPE_BASE), jnp.arange(half, dtype=F32) * (-2.0 / LANE))
+    freq = jnp.concatenate([freq, freq]).reshape(1, LANE)
+    step = SUB * GRP
+    whole = lambda shape: pl.BlockSpec(shape, lambda i, *_: (0,) * len(shape))
+    cache = pl.BlockSpec((step, seq, LANE), lambda i, *_: (i, 0, 0))
+    hbm = pl.BlockSpec(memory_space=pl.ANY)
+    k3, v3 = k_blk.reshape(rows, seq, LANE), v_blk.reshape(rows, seq, LANE)
+    packed, ko, vo = pl.pallas_call(
+        attend_kernel,
+        name="attend",
+        grid_spec=pltpu.PrefetchScalarGridSpec(
+            num_scalar_prefetch=1,
+            grid=(rows // step,),
+            in_specs=[whole((rows // LANE, LANE)), whole((rows, width)), whole((1, width)), whole((1, LANE)), cache, cache, hbm, hbm, hbm],
+            out_specs=[pl.BlockSpec((step, hd + LANE), lambda i, *_: (i, 0)), cache, cache],
+            scratch_shapes=[
+                pltpu.VMEM((width, hd + 2 * LANE), BF16),
+                pltpu.VMEM((hd // LANE, rows, LANE), BF16),
+                pltpu.VMEM((rows, LANE), F32),
+                pltpu.VMEM((rows, LANE), F32),
+                pltpu.VMEM((rows, LANE), jnp.int32),
+                pltpu.SemaphoreType.DMA((8,)),
+            ],
+        ),
+        out_shape=[
+            jax.ShapeDtypeStruct((rows, hd + LANE), F32),
+            jax.ShapeDtypeStruct(k3.shape, BF16),
+            jax.ShapeDtypeStruct(v3.shape, BF16),
+        ],
+        compiler_params=pltpu.CompilerParams(dimension_semantics=("arbitrary",), vmem_limit_bytes=40 * 2**20),
+    )(seq_lens, seq_lens.reshape(rows // LANE, LANE), x_tok, g.reshape(1, -1), freq, k3, v3, wq, wk, wv)
+    return packed, ko.reshape(k_blk.shape), vo.reshape(v_blk.shape)
+
+
 def solution(mesh):
     cache_spec = P(None, "sp", "tp", None)
     col_spec = P(None, "tp")
@@ -337,36 +466,11 @@
     full_spec = P()
 
     def local_step(x_tok, seq_lens, k_blk, v_blk, g_attn, wq_loc, wk_loc, wv_loc, wo_loc, g_mlp, wg_loc, wu_loc, wd_loc):
-        batch_rows, seq_blk, kv_loc, head_dim = k_blk.shape
-        q_loc = wq_loc.shape[1] // head_dim
-        groups = q_loc // kv_loc
         x, z, y, c = coords()
         w = x_tok.shape[1] // NX
         res = lax.dynamic_slice(x_tok, (row_chunk(z, y, c) * 8, x * w), (8, w)).astype(F32)
-        x_norm = rms_norm(x_tok, g_attn)
-        q_new = jnp.dot(x_norm, wq_loc, preferred_element_type=F32).astype(BF16).reshape(batch_rows, q_loc, head_dim)
-        k_new = jnp.dot(x_norm, wk_loc, preferred_element_type=F32).astype(BF16).reshape(batch_rows, kv_loc, head_dim)
-        v_new = jnp.dot(x_norm, wv_loc, preferred_element_type=F32).astype(BF16).reshape(batch_rows, kv_loc, head_dim)
-        q_rot = apply_rope(q_new, seq_lens)
-        k_rot = apply_rope(k_new, seq_lens)
-        local_pos = lax.axis_index("sp") * seq_blk + jnp.arange(seq_blk)
-        is_new = (local_pos[None, :] == seq_lens[:, None])[:, :, None, None]
-        k_out = jnp.where(is_new, k_rot[:, None], k_blk)
-        v_out = jnp.where(is_new, v_new[:, None], v_blk)
-        q_grp = q_rot.reshape(batch_rows, kv_loc, groups, head_dim)
-        scores = jnp.einsum("bkgd,bskd->bkgs", q_grp, k_out, preferred_element_type=F32) * (head_dim ** -0.5)
-        is_valid = (local_pos[None, :] <= seq_lens[:, None])[:, None, None, :]
-        masked = jnp.where(is_valid, scores, -1e30)
-        blk_max = jnp.max(masked, axis=-1, keepdims=True)
-        weights = jnp.where(is_valid, jnp.exp(masked - blk_max), 0.0)
-        blk_sum = jnp.sum(weights, axis=-1, keepdims=True)
-        blk_mix = jnp.einsum("bkgs,bskd->bkgd", weights.astype(BF16), v_out, preferred_element_type=F32)
-        half = LANE // 2
-        pad = jnp.zeros((batch_rows, half - q_loc), F32)
-        packed = jnp.concatenate(
-            [blk_mix.reshape(batch_rows, q_loc * head_dim), blk_max.reshape(batch_rows, q_loc), pad, blk_sum.reshape(batch_rows, q_loc), pad], axis=1
-        )
-        attn_out = combine(packed, q_loc)
+        packed, k_out, v_out = attend(x_tok, seq_lens, k_blk, v_blk, g_attn, wq_loc, wk_loc, wv_loc)
+        attn_out = combine(packed, wq_loc.shape[1] // LANE)
         part = jnp.dot(attn_out, wo_loc, preferred_element_type=F32)
         hid = gather_hidden(part, res)
         mlp_part = mlp(hid, g_mlp, wg_loc, wu_loc, wd_loc)

time: 137 us -> 134 us (0.978)
  Pallas kernels: 95.6 us -> 112 us
  other arithmetic: 15.9 us -> 4.9 us
  matrix products: 14.6 us -> 4.43 us
  local copies, waits for them, and re-layouts: 8.92 us -> 11.9 us
    pallas_call x0 -> x1, Pallas kernels: none -> 17.7 us  [attend(): pl.pallas_call(attend_kernel, name='attend', grid_spec=pltpu.PrefetchScal...]
    dot_general x5 -> x0, matrix products: 10.2 us -> none  [the longest x1 5.87 us: local_step(): jnp.dot(x_norm, wq_loc, preferred_element_type=F32).astype(BF16)]
    unnamed x28 -> x18, local copies, waits for them, and re-layouts: 4.07 us -> 10.5 us
    select_n x1 -> x0, other arithmetic: 4.21 us -> none  [local_step(): k_out = jnp.where(is_new, k_rot[:, None], k_blk)]
    reduce_sum x2 -> x0, other arithmetic: 2.69 us -> none  [the longest x1 1.94 us: rms_norm(): jnp.mean(x_f32 * x_f32, axis=-1, keepdims=True) + NORM_EPS]
    concatenate x2 -> x0, local copies, waits for them, and re-layouts: 1.93 us -> none  [the longest x1 1.21 us: local_step(): jnp.concatenate([blk_mix.reshape(batch_rows, q_loc * head_dim), blk_max.r...]
    pallas_call x1, Pallas kernels: 41.8 us -> 40 us  [gather_output(): pl.pallas_call(output_kernel, name='gather_output', out_shape=jax.ShapeDt...]
    convert_element_type x2 -> x0, other arithmetic: 1.54 us -> none  [the longest x1 0.83 us: apply_rope(): angles = positions.astype(F32)[:, None, None] * inv_freq]
where the time goes in v2:
time: 134 us
  Pallas kernels  112 us (84%)
  local copies, waits for them, and re-layouts  11.9 us (9%)
  other arithmetic  4.9 us (4%)
  matrix products  4.43 us (3%)
    pallas_call x1, Pallas kernels, gather_output(): pl.pallas_call(output_kernel, name='gather_output', out_shape=jax.ShapeDt...  40 us
    pallas_call x1, Pallas kernels, combine(): pl.pallas_call(combine_kernel, name='combine', out_shape=jax.ShapeDtypeSt...  28.6 us
    pallas_call x1, Pallas kernels, attend(): pl.pallas_call(attend_kernel, name='attend', grid_spec=pltpu.PrefetchScal...  17.7 us
    pallas_call x1, Pallas kernels, gather_hidden(): pl.pallas_call(hidden_kernel, name='gather_hidden', out_shape=jax.ShapeDt...  15.4 us
    unnamed x18, local copies, waits for them, and re-layouts  10.5 us
    pallas_call x1, Pallas kernels, mlp(): pl.pallas_call(mlp_kernel, name='mlp', out_shape=jax.ShapeDtypeStruct((ro...  9.84 us
    dot_general x1, matrix products, local_step(): part = jnp.dot(attn_out, wo_loc, preferred_element_type=F32)  4.43 us
    convert_element_type x1, other arithmetic, local_step(): y_out = buf.transpose(0, 1, 2, 4, 3, 5).reshape(x_tok.shape).astype(BF16)  3.49 us

profile of v2, /device:TPU:1, one launch (start us, length us, event | category | flops | bytes accessed | tf_op | source)
XLA Modules:
  0.0 133.5 jit_solution(13970200777549658881)
XLA Ops:
  0.7 0.1 maximum_bitcast_fusion.freq_ref
  0.8 0.7 reshape.33.g_ref
  1.5 0.7 reshape.37.g_ref
  2.2 1.3 dynamic-slice_convert_fusion.res_ref
  3.5 0.0 copy-start.1
  3.5 1.6 %copy-done.1 = bf16[256,32,1,128]{3,1,2,0:T(8,128)(2,1)S(1)} copy-done((bf16[256,32,1,128]{3,1,2,0:T(8,128)(2,1)S(1)}, bf16[256,32,1,128]{3,1,2,0:T(8,128)(2,1)}, u32[]{:S(2)}) %copy-start.1) | copy-done | bytes 2097176
  5.1 0.0 copy-start.2
  5.1 1.6 %copy-done.2 = bf16[256,32,1,128]{3,1,2,0:T(8,128)(2,1)S(1)} copy-done((bf16[256,32,1,128]{3,1,2,0:T(8,128)(2,1)S(1)}, bf16[256,32,1,128]{3,1,2,0:T(8,128)(2,1)}, u32[]{:S(2)}) %copy-start.2) | copy-done | bytes 2097176
  6.7 0.0 copy-start.3
  6.7 1.5 %copy-done.3 = bf16[256,3584]{1,0:T(8,128)(2,1)S(1)} copy-done((bf16[256,3584]{1,0:T(8,128)(2,1)S(1)}, bf16[256,3584]{1,0:T(8,128)(2,1)}, u32[]{:S(2)}) %copy-start.3) | copy-done | bytes 1835032
  8.2 0.0 copy-start.6
  8.2 1.2 copy-done.6
  9.4 0.0 copy-start.7
  9.4 1.2 copy-done.7
  10.6 0.0 copy-start.8
  10.6 0.7 copy-done.8
  11.2 17.7 %attend.1 = (f32[256,1024]{1,0:T(8,128)S(1)}, bf16[256,32,128]{2,1,0:T(8,128)(2,1)}, bf16[256,32,128]{2,1,0:T(8,128)(2,1)}) custom-call(s32[256]{0:T(256)S(1)} %copy-done.8, s32[2,128]{1,0:T(2,128)S(1)} %bitcast.18, bf16[256,3584]{1,0:T(8,128)(2,1)S(1)} %copy-done.3, bf16[1,3584]{1,0:T(2,128)(2,1)S(1)} %reshape.33.g_ref, ...), custom_call_target="tpu_custom_call" | custom-call | tf_op jit(solution)/shard_map/attend/pallas_call | solution.py:435
  29.0 0.0 copy-start.5
  29.0 1.0 copy-done.5
  29.9 28.6 %combine.1 = bf16[8,896]{1,0:T(8,128)(2,1)} custom-call(f32[256,1024]{1,0:T(8,128)} %copy-done.5), custom_call_target="tpu_custom_call" | custom-call | tf_op jit(solution)/shard_map/combine/pallas_call | solution.py:90
  58.5 4.4 %fusion.part_ref = f32[8,3584]{1,0:T(8,128)} fusion(bf16[8,896]{1,0:T(8,128)(2,1)} %combine.1, bf16[896,3584]{1,0:T(8,128)(2,1)} %param.21), kind=kOutput, calls=%fused_computation.3 | convolution fusion | flops 51380224 | bytes 6551552 | tf_op jit(solution)/shard_map/dot_general | solution.py:474
  62.9 15.4 %gather_hidden.1.hid_ref = f32[32,3584]{1,0:T(8,128)} custom-call(f32[8,3584]{1,0:T(8,128)} %fusion.part_ref, f32[8,896]{1,0:T(8,128)} %dynamic-slice_convert_fusion.res_ref), custom_call_target="tpu_custom_call" | custom-call | tf_op jit(solution)/shard_map/gather_hidden/pallas_call | solution.py:143
  78.3 0.0 copy-start
  78.3 1.0 copy-done
  79.4 9.8 %mlp.1.part_ref = f32[32,3584]{1,0:T(8,128)S(1)} custom-call(f32[32,3584]{1,0:T(8,128)S(1)} %copy-done, bf16[1,3584]{1,0:T(2,128)(2,1)S(1)} %reshape.37.g_ref, bf16[3584,4736]{1,0:T(8,128)(2,1)} %wg_hbm.1, bf16[3584,4736]{1,0:T(8,128)(2,1)} %wu_hbm.1, bf16[4736,3584]{1,0:T(8,128)(2,1)} %wd_hbm.1), custom_call_target="tpu_custom_call" | custom-call | flops 880803840 | bytes 27525120 | tf_op jit(solution)/shard_map/mlp/pallas_call | solution.py:210
  89.2 0.0 copy-start.4
  89.2 0.8 copy-done.4
  90.0 40.0 %gather_output.1 = f32[4,2,4,4,8,896]{5,4,3,2,1,0:T(8,128)} custom-call(f32[32,3584]{1,0:T(8,128)} %copy-done.4, f32[32,3584]{1,0:T(8,128)} %gather_hidden.1.hid_ref), custom_call_target="tpu_custom_call" | custom-call | tf_op jit(solution)/shard_map/gather_output/pallas_call | solution.py:298
  130.0 3.5 %convert_element_type.13 = bf16[4,2,4,4,8,896]{5,4,3,2,1,0:T(8,128)(2,1)} convert(f32[4,2,4,4,8,896]{5,4,3,2,1,0:T(8,128)} %gather_output.1) | non-fusion elementwise | flops 917504 | bytes 5505024 | tf_op jit(solution)/shard_map/convert_element_type | solution.py:478
  (1 shorter events, 0.0 us)
Async XLA Ops:
  3.5 1.6 %copy-start.1 = (bf16[256,32,1,128]{3,1,2,0:T(8,128)(2,1)S(1)}, bf16[256,32,1,128]{3,1,2,0:T(8,128)(2,1)}, u32[]{:S(2)}) copy-start(bf16[256,32,1,128]{3,1,2,0:T(8,128)(2,1)} %param.15) | copy-start | bytes 6291460
  5.1 1.6 %copy-start.2 = (bf16[256,32,1,128]{3,1,2,0:T(8,128)(2,1)S(1)}, bf16[256,32,1,128]{3,1,2,0:T(8,128)(2,1)}, u32[]{:S(2)}) copy-start(bf16[256,32,1,128]{3,1,2,0:T(8,128)(2,1)} %param.16) | copy-start | bytes 6291460
  6.7 1.5 %copy-start.3 = (bf16[256,3584]{1,0:T(8,128)(2,1)S(1)}, bf16[256,3584]{1,0:T(8,128)(2,1)}, u32[]{:S(2)}) copy-start(bf16[256,3584]{1,0:T(8,128)(2,1)} %x_ref.1) | copy-start | bytes 5505028
  8.2 1.2 copy-start.6
  9.4 1.2 copy-start.7
  10.6 0.7 copy-start.8
  29.0 1.0 copy-start.5
  78.3 1.0 copy-start
  89.2 0.8 copy-start.4

commit v3 on v0

v3 whole, which is shorter than its diff:
```python
import functools

import jax
import jax.numpy as jnp
from jax import lax
from jax.experimental import pallas as pl
from jax.experimental.pallas import tpu as pltpu
from jax.sharding import PartitionSpec as P

ROPE_BASE = 500000.0
NORM_EPS = 1e-5
MESH = pl.DeviceIdType.MESH
F32 = jnp.float32
BF16 = jnp.bfloat16
NX, NZ, NY, NC = 4, 4, 4, 2
LANE = 128
VMEM_ALL = 67043328


def coords():
    s = lax.axis_index("sp")
    return lax.axis_index("tp"), s // (NY * NC), (s // NC) % NY, s % NC


def dev(x, z, y, c):
    return (x, (z * NY + y) * NC + c)


def turn(v, d, n):
    return lax.rem(v + d, n)


def entry_barrier(peers):
    barrier = pltpu.get_barrier_semaphore()
    for peer in peers:
        pl.semaphore_signal(barrier, inc=1, device_id=peer, device_id_type=MESH)
    pl.semaphore_wait(barrier, len(peers))


def remote(src, dst, send_sem, recv_sem, peer):
    return pltpu.make_async_remote_copy(
        src_ref=src, dst_ref=dst, send_sem=send_sem, recv_sem=recv_sem, device_id=peer, device_id_type=MESH
    )


XY = [(dx, dy) for dx in range(4) for dy in range(4)][1:]
WIN = 256


def layer_kernel(
    in_ref, res_ref, g_ref, wo_hbm, wg_hbm, wu_hbm, wd_hbm, out_ref,
    swap, merged, slots, part, xslots, chunk, hid, hn, acc, cslot, buf,
    wg, wu, wg_t, wu_t, wd,
    w_sem, swap_sem, rs_send, rs_recv, xs_send, xs_recv, ag_send, ag_recv, fw_send, fw_recv,
    c_sem, xo_send, xo_recv, p1_send, p1_recv, p2_send, p2_recv, cc_send, cc_recv,
):
    x, z, y, c = coords()
    w = chunk.shape[1]
    heads = w // LANE
    half = LANE // 2
    mate = turn(c, 1, NC)
    partner = dev(x, z, y, mate)
    steps = wg.shape[0]
    wide = steps * WIN
    ff = wg_hbm.shape[1]
    window = wide + LANE
    first = pl.multiple_of(c * (ff - window), LANE)
    keep = wd.shape[0] - wo_hbm.shape[0]

    def fetch(i):
        cols = pl.ds(pl.multiple_of(first + i * WIN, LANE), WIN)
        return (
            pltpu.make_async_copy(wg_hbm.at[:, cols], wg.at[i], w_sem.at[0, i]),
            pltpu.make_async_copy(wu_hbm.at[:, cols], wu.at[i], w_sem.at[1, i]),
        )

    def fetch_down(i):
        rows = pl.ds(pl.multiple_of(first + i * WIN, LANE), WIN)
        here = pl.ds(pl.multiple_of(i * WIN, LANE), WIN)
        return pltpu.make_async_copy(wd_hbm.at[rows, :], wd.at[here, :], w_sem.at[2, i])

    tail = pl.ds(pl.multiple_of(first + wide, LANE), LANE)
    tails = (
        pltpu.make_async_copy(wg_hbm.at[:, tail], wg_t, w_sem.at[0, steps]),
        pltpu.make_async_copy(wu_hbm.at[:, tail], wu_t, w_sem.at[1, steps]),
        pltpu.make_async_copy(wd_hbm.at[tail, :], wd.at[wide:, :], w_sem.at[2, steps]),
    )
    get_wo = pltpu.make_async_copy(wo_hbm, wd.at[keep:, :], w_sem.at[3, 0])
    n_keep = keep // WIN

    planes = [
        [(turn(x, a, NX), z, turn(y, b, NY)) for a, b in XY],
        [(x, turn(z, a, NZ), turn(y, b, NY)) for a, b in XY],
        [(turn(x, a, NX), turn(z, b, NZ), y) for a, b in XY],
    ]
    near = planes[0] + [(x, turn(z, a, NZ), turn(y, b, NY)) for a in range(1, NZ) for b in range(NY)]
    near += [(turn(x, a, NX), turn(z, b, NZ), y) for a in range(1, NX) for b in range(1, NZ)]
    entry_barrier([dev(*p, c) for p in near] + [partner])

    give = remote(in_ref.at[:, mate], swap, swap_sem.at[0], swap_sem.at[1], partner)
    give.start()
    get_wo.start()
    give.wait_recv()
    low = lax.broadcasted_iota(jnp.int32, (8, LANE), 1) < half

    def pair(g):
        s1, s2 = in_ref[g, c, :, w:], swap[g, :, w:]
        top = jnp.maximum(s1, s2)
        f1, f2 = jnp.exp(s1 - top), jnp.exp(s2 - top)
        total = pltpu.roll(f1, half, 1) * s1 + pltpu.roll(f2, half, 1) * s2
        mix = []
        for h in range(heads):
            cut = slice(h * LANE, (h + 1) * LANE)
            mix.append(f1[:, h:h + 1] * in_ref[g, c, :, cut] + f2[:, h:h + 1] * swap[g, :, cut])
        return mix, jnp.where(low, top, total)

    rs = []
    for k, (_, pz, py) in enumerate(planes[1]):
        g = pz * NY + py
        mix, stats = pair(g)
        for h in range(heads):
            merged[k, :, h * LANE:(h + 1) * LANE] = mix[h]
        merged[k, :, w:] = stats
        copy = remote(merged.at[k], slots.at[k], rs_send.at[k], rs_recv.at[k], dev(x, pz, py, c))
        copy.start()
        rs.append(copy)
    for i in range(n_keep):
        for copy in fetch(i) + (fetch_down(i),):
            copy.start()
    for i in range(n_keep, steps):
        for copy in fetch(i):
            copy.start()
    for copy in tails[:2]:
        copy.start()
    own_mix, own_stats = pair(z * NY + y)
    for copy in rs:
        copy.wait_recv()
    top = own_stats
    for k in range(len(rs)):
        top = jnp.maximum(top, slots[k, :, w:])

    def add(stats, mix, acc_mix, total):
        factor = jnp.exp(stats - top)
        total = total + pltpu.roll(factor, half, 1) * stats
        return [acc_mix[h] + factor[:, h:h + 1] * mix[h] for h in range(heads)], total

    mixed, total = add(own_stats, own_mix, [jnp.zeros((8, LANE), F32)] * heads, jnp.zeros((8, LANE), F32))
    for k in range(len(rs)):
        mix = [slots[k, :, h * LANE:(h + 1) * LANE] for h in range(heads)]
        mixed, total = add(slots[k, :, w:], mix, mixed, total)
    attn = jnp.concatenate([mixed[h] / total[:, half + h:half + h + 1] for h in range(heads)], axis=1).astype(BF16)

    get_wo.wait()
    for n in range(0, part.shape[1], 4 * LANE):
        part[:, n:n + 4 * LANE] = jnp.dot(attn, wd[keep:, n:n + 4 * LANE], preferred_element_type=F32)
    my_cols = pl.ds(pl.multiple_of(x * w, LANE), w)
    my_rows = pl.ds(pl.multiple_of(c * 8, 8), 8)
    line = [turn(x, k, NX) for k in range(1, NX)]
    cols = [pl.ds(pl.multiple_of(px * w, LANE), w) for px in line]
    xs = []
    for k, px in enumerate(line):
        copy = remote(part.at[:, cols[k]], xslots.at[k], xs_send.at[k], xs_recv.at[k], dev(px, z, y, c))
        copy.start()
        xs.append(copy)
    for i in range(n_keep, steps):
        fetch_down(i).start()
    tails[2].start()
    sums = part[:, my_cols]
    for k, copy in enumerate(xs):
        copy.wait_recv()
        sums = sums + xslots[k]
    hidden = (res_ref[...] + sums).astype(BF16).astype(F32)
    chunk[...] = hidden
    ag = []
    for k, px in enumerate(line):
        copy = remote(chunk, hid.at[my_rows, my_cols], ag_send.at[k], ag_recv.at[k], dev(px, z, y, c))
        copy.start()
        ag.append(copy)
    fw = [remote(chunk, hid.at[my_rows, my_cols], fw_send.at[3], fw_recv.at[3], partner)]
    fw[0].start()
    hid[my_rows, my_cols] = hidden
    for k, copy in enumerate(ag):
        copy.wait_recv()
        block = hid.at[my_rows, cols[2 - k]]
        copy = remote(block, block, fw_send.at[k], fw_recv.at[k], partner)
        copy.start()
        fw.append(copy)
    for copy in fw:
        copy.wait_recv()

    h32 = hid[...]
    inv = lax.rsqrt(jnp.mean(h32 * h32, axis=-1, keepdims=True) + NORM_EPS)
    hn[...] = (h32 * inv * g_ref[...].astype(F32)).astype(BF16)
    acc[...] = jnp.zeros_like(acc)
    mid = (ff // LANE + 1) // 2 * LANE

    def gated(gate, up, start):
        gate = gate.astype(BF16).astype(F32)
        up = up.astype(BF16).astype(F32)
        col = lax.broadcasted_iota(jnp.int32, gate.shape, 1) + start
        lo = c * mid
        act = jax.nn.silu(gate) * up
        return jnp.where((col >= lo) & (col < mid + c * ff), act, 0.0).astype(BF16)

    def mlp_step(i, carry):
        cg, cu = fetch(i)
        cg.wait()
        gate = jnp.dot(hn[...], wg[i], preferred_element_type=F32)
        cu.wait()
        up = jnp.dot(hn[...], wu[i], preferred_element_type=F32)
        act = gated(gate, up, first + i * WIN)
        fetch_down(i).wait()
        here = pl.ds(pl.multiple_of(i * WIN, LANE), WIN)
        acc[...] += jnp.dot(act, wd[here, :], preferred_element_type=F32)
        return carry

    lax.fori_loop(0, steps, mlp_step, 0)
    tails[0].wait()
    gate = jnp.dot(hn[...], wg_t[...], preferred_element_type=F32)
    tails[1].wait()
    up = jnp.dot(hn[...], wu_t[...], preferred_element_type=F32)
    act = gated(gate, up, first + wide)
    tails[2].wait()
    acc[...] += jnp.dot(act, wd[wide:, :], preferred_element_type=F32)

    mate_rows = pl.ds(pl.multiple_of(mate * 8, 8), 8)
    back = remote(acc.at[mate_rows, :], cslot, c_sem.at[0], c_sem.at[1], partner)
    back.start()
    for copy in xs:
        copy.wait_send()
    back.wait_recv()
    part[...] = acc[my_rows, :] + cslot[...]
    xo = []
    for k, px in enumerate(line):
        copy = remote(part.at[:, cols[k]], xslots.at[k + 3], xo_send.at[k], xo_recv.at[k], dev(px, z, y, c))
        copy.start()
        xo.append(copy)
    sums = part[:, my_cols]
    for k, copy in enumerate(xo):
        copy.wait_recv()
        sums = sums + xslots[k + 3]
    out = (hidden + sums).astype(BF16).astype(F32)
    for copy in ag + fw[:1]:
        copy.wait_send()
    chunk[...] = out

    cut = [(0, 2 * LANE), (2 * LANE, 2 * LANE), (4 * LANE, w - 4 * LANE)]
    p1 = []
    for p, (lo, n) in enumerate(cut):
        for k, peer in enumerate(planes[p]):
            src, dst = chunk.at[:, lo:lo + n], buf.at[z, y, c, x, :, lo:lo + n]
            copy = remote(src, dst, p1_send.at[p, k], p1_recv.at[p, k], dev(*peer, c))
            copy.start()
            p1.append(copy)
    buf[z, y, c, x] = out

    def block(p, v, h):
        lo, n = cut[p]
        cols_p = slice(lo, lo + n)
        two = slice(2 * h, 2 * h + 2)
        return [buf.at[v, two, c, :, :, cols_p], buf.at[two, :, c, v, :, cols_p], buf.at[two, v, c, :, :, cols_p]][p]

    here = [z, x, y]
    up1 = [dev(x, turn(z, 1, 4), y, c), dev(turn(x, 1, 4), z, y, c), dev(x, z, turn(y, 1, 4), c)]
    dn1 = [dev(x, turn(z, 3, 4), y, c), dev(turn(x, 3, 4), z, y, c), dev(x, z, turn(y, 3, 4), c)]
    done = []

    def send(p, v, h, to, i):
        copy = remote(block(p, v, h), block(p, v, h), p2_send.at[p, i], p2_recv.at[p, i], to)
        copy.start()
        done.append(copy)
        return copy

    def across(p, v, h, i):
        copy = remote(block(p, v, h), block(p, v, h), cc_send.at[p, i], cc_recv.at[p, i], partner)
        copy.start()
        done.append(copy)
        return copy

    direct, relayed, crossed = [], [], []
    for p in range(3):
        for copy in p1[p * 15:(p + 1) * 15]:
            copy.wait_recv()
        v = here[p]
        direct.append([send(p, v, 0, up1[p], 0), send(p, v, 1, dn1[p], 1), send(p, v, 1, up1[p], 2), send(p, v, 0, dn1[p], 3)])
        crossed += [across(p, v, 0, 0), across(p, v, 1, 1)]
    for p in range(3):
        below, above = turn(here[p], 3, 4), turn(here[p], 1, 4)
        direct[p][0].wait_recv()
        far = [send(p, below, 0, up1[p], 4)]
        direct[p][1].wait_recv()
        far += [send(p, above, 1, dn1[p], 5)]
        relayed.append(far)
        crossed += [across(p, below, 0, 2), across(p, above, 1, 3)]
    for p in range(3):
        below, above = turn(here[p], 3, 4), turn(here[p], 1, 4)
        direct[p][2].wait_recv()
        crossed += [across(p, below, 1, 4)]
        direct[p][3].wait_recv()
        crossed += [across(p, above, 0, 5)]
    for p in range(3):
        far = turn(here[p], 2, 4)
        relayed[p][0].wait_recv()
        crossed += [across(p, far, 0, 6)]
        relayed[p][1].wait_recv()
        crossed += [across(p, far, 1, 7)]
    for copy in crossed:
        copy.wait_recv()
    for a in range(NZ):
        for b in range(NY):
            for e in range(NC):
                r = ((a * NY + b) * NC + e) * 8
                for d in range(NX):
                    out_ref[r:r + 8, d * w:(d + 1) * w] = buf[a, b, e, d].astype(BF16)
    for copy in [give, back] + rs + fw[1:] + xo + p1 + done:
        copy.wait_send()


def layer(packed, res, g, wo, wg, wu, wd, rows):
    packed = packed.reshape(NZ * NY, NC, 8, packed.shape[1])
    width = wo.shape[1]
    w = width // NX
    steps = ((wg.shape[1] // LANE + 1) // 2 * LANE) // WIN
    sem = pltpu.SemaphoreType.DMA
    vmem = pl.BlockSpec(memory_space=pltpu.VMEM)
    hbm = pl.BlockSpec(memory_space=pl.ANY)
    return pl.pallas_call(
        layer_kernel,
        name="layer",
        out_shape=jax.ShapeDtypeStruct((rows, width), BF16),
        in_specs=[vmem] * 3 + [hbm] * 4,
        out_specs=vmem,
        scratch_shapes=[
            pltpu.VMEM((NZ * NY, 8, packed.shape[3]), F32),
            pltpu.VMEM((15, 8, packed.shape[3]), F32),
            pltpu.VMEM((15, 8, packed.shape[3]), F32),
            pltpu.VMEM((8, width), F32),
            pltpu.VMEM((6, 8, w), F32),
            pltpu.VMEM((8, w), F32),
            pltpu.VMEM((8 * NC, width), F32),
            pltpu.VMEM((8 * NC, width), BF16),
            pltpu.VMEM((8 * NC, width), F32),
            pltpu.VMEM((8, width), F32),
            pltpu.VMEM((NZ, NY, NC, NX, 8, w), F32),
            pltpu.VMEM((steps, width, WIN), BF16),
            pltpu.VMEM((steps, width, WIN), BF16),
            pltpu.VMEM((width, LANE), BF16),
            pltpu.VMEM((width, LANE), BF16),
            pltpu.VMEM((steps * WIN + LANE, width), BF16),
            sem((4, steps + 1)),
            sem((2,)), sem((15,)), sem((15,)), sem((3,)), sem((3,)), sem((3,)), sem((3,)), sem((4,)), sem((4,)),
            sem((2,)), sem((3,)), sem((3,)), sem((3, 15)), sem((3, 15)), sem((3, 6)), sem((3, 6)), sem((3, 8)), sem((3, 8)),
        ],
        compiler_params=pltpu.CompilerParams(collective_id=0, has_side_effects=True, vmem_limit_bytes=VMEM_ALL),
    )(packed, res, g.reshape(1, -1), wo, wg, wu, wd)


GRP = 16
SUB = 4


def attend_kernel(lens_ref, lens_row, x_ref, g_ref, freq_ref, k_ref, v_ref, wq_hbm, wk_hbm, wv_hbm, pack_ref, ko_ref, vo_ref, w, q, knew, vnew, pos, sem):
    step = pl.program_id(0)
    rows = x_ref.shape[0]
    heads = wq_hbm.shape[1] // LANE
    seq = k_ref.shape[1]
    half = LANE // 2
    hd = heads * LANE
    base = lax.axis_index("sp") * seq

    @pl.when(step == 0)
    def project():
        odd = hd % (2 * LANE)
        cuts = [(i, 2 * LANE) for i in range(0, hd - odd, 2 * LANE)]
        copies = [[pltpu.make_async_copy(wq_hbm.at[:, a:a + n], w.at[:, a:a + n], sem.at[i])] for i, (a, n) in enumerate(cuts)]
        n = len(cuts)
        last = [
            pltpu.make_async_copy(wq_hbm.at[:, hd - odd:], w.at[:, hd - odd:hd], sem.at[n]),
            pltpu.make_async_copy(wk_hbm, w.at[:, hd:hd + LANE], sem.at[n + 1]),
        ]
        copies += [last, [pltpu.make_async_copy(wv_hbm, w.at[:, hd + LANE:], sem.at[n + 2])]]
        cuts += [(hd - odd, odd + LANE), (hd + LANE, LANE)]
        for group in copies:
            for copy in group:
                copy.start()
        x32 = x_ref[...].astype(F32)
        inv = lax.rsqrt(jnp.mean(x32 * x32, axis=-1, keepdims=True) + NORM_EPS)
        u = (x32 * inv * g_ref[...].astype(F32)).astype(BF16)
        eye = lax.broadcasted_iota(jnp.int32, (LANE, LANE), 0) == lax.broadcasted_iota(jnp.int32, (LANE, LANE), 1)
        cols = []
        for i in range(rows // LANE):
            line = lens_row[i:i + 1, :].astype(F32)
            col = jnp.sum(jnp.where(eye, line, 0.0), axis=1, keepdims=True)
            pos[i * LANE:(i + 1) * LANE, :] = jnp.broadcast_to(col, (LANE, LANE)).astype(jnp.int32)
            cols.append(col)
        low = lax.broadcasted_iota(jnp.int32, (LANE, LANE), 1) < half
        angles = jnp.where(low, cols[0], cols[1]) * freq_ref[...]
        cos = jnp.cos(angles)
        sin = jnp.sin(angles)
        cos_r = pltpu.roll(cos, half, 1)
        sin_r = pltpu.roll(sin, half, 1)
        cos_t = jnp.concatenate([jnp.where(low, cos, cos_r), jnp.where(low, cos_r, cos)], axis=0)
        sin_t = jnp.concatenate([jnp.where(low, -sin, sin_r), jnp.where(low, -sin_r, sin)], axis=0)
        for group, (a, n) in zip(copies, cuts):
            for copy in group:
                copy.wait()
            out = jnp.dot(u, w[:, a:a + n], preferred_element_type=F32).astype(BF16).astype(F32)
            for j in range(0, n, LANE):
                h = (a + j) // LANE
                part = out[:, j:j + LANE]
                if h <= heads:
                    part = (part * cos_t + pltpu.roll(part, half, 1) * sin_t).astype(BF16)
                if h < heads:
                    q[h] = part
                elif h == heads:
                    knew[...] = part.astype(F32)
                else:
                    vnew[...] = part

    first = step * SUB * GRP
    line = lax.broadcasted_iota(jnp.int32, (seq, LANE), 0)
    for b in range(SUB * GRP):
        here = line == lens_ref[first + b] - base
        k_row = knew[pl.ds(first + b, 1), :]
        v_row = vnew[pl.ds(first + b, 1), :]
        ko_ref[b] = jnp.where(here, k_row, k_ref[b].astype(F32)).astype(BF16)
        vo_ref[b] = jnp.where(here, v_row, v_ref[b].astype(F32)).astype(BF16)
    span = GRP * seq
    col = lax.broadcasted_iota(jnp.int32, (GRP, span), 1)
    own = (col // seq) == lax.broadcasted_iota(jnp.int32, (GRP, span), 0)
    where_at = base + col % seq
    lane = lax.broadcasted_iota(jnp.int32, (GRP, LANE), 1)
    for s in range(SUB):
        at = pl.ds(pl.multiple_of(first + s * GRP, GRP), GRP)
        block = slice(s * GRP, (s + 1) * GRP)
        qs = jnp.concatenate([q[h, at, :] for h in range(heads)], axis=0)
        ks = ko_ref[block].reshape(span, LANE)
        vs = vo_ref[block].reshape(span, LANE)
        p = jnp.concatenate([pos[at, :]] * (span // LANE), axis=1)
        valid = own & (where_at <= p)
        valid = jnp.concatenate([valid.astype(F32)] * heads, axis=0) > 0.5
        scores = lax.dot_general(qs, ks, (((1,), (1,)), ((), ())), preferred_element_type=F32) * (LANE ** -0.5)
        scores = jnp.where(valid, scores, -1e30)
        top = jnp.max(scores, axis=1, keepdims=True)
        wt = jnp.where(valid, jnp.exp(scores - top), 0.0)
        tot = jnp.sum(wt, axis=1, keepdims=True)
        mix = jnp.dot(wt.astype(BF16), vs, preferred_element_type=F32)
        stats = jnp.zeros((GRP, LANE), F32)
        for h in range(heads):
            part = slice(h * GRP, (h + 1) * GRP)
            pack_ref[block, h * LANE:(h + 1) * LANE] = mix[part]
            stats = jnp.where(lane == h, top[part], stats)
            stats = jnp.where(lane == half + h, tot[part], stats)
        pack_ref[block, hd:] = stats


def attend(x_tok, seq_lens, k_blk, v_blk, g, wq, wk, wv):
    rows, width = x_tok.shape
    seq = k_blk.shape[1]
    hd = wq.shape[1]
    half = LANE // 2
    freq = jnp.power(F32(ROPE_BASE), jnp.arange(half, dtype=F32) * (-2.0 / LANE))
    freq = jnp.concatenate([freq, freq]).reshape(1, LANE)
    step = SUB * GRP
    whole = lambda shape: pl.BlockSpec(shape, lambda i, *_: (0,) * len(shape))
    cache = pl.BlockSpec((step, seq, LANE), lambda i, *_: (i, 0, 0))
    hbm = pl.BlockSpec(memory_space=pl.ANY)
    k3, v3 = k_blk.reshape(rows, seq, LANE), v_blk.reshape(rows, seq, LANE)
    packed, ko, vo = pl.pallas_call(
        attend_kernel,
        name="attend",
        grid_spec=pltpu.PrefetchScalarGridSpec(
            num_scalar_prefetch=1,
            grid=(rows // step,),
            in_specs=[whole((rows // LANE, LANE)), whole((rows, width)), whole((1, width)), whole((1, LANE)), cache, cache, hbm, hbm, hbm],
            out_specs=[pl.BlockSpec((step, hd + LANE), lambda i, *_: (i, 0)), cache, cache],
            scratch_shapes=[
                pltpu.VMEM((width, hd + 2 * LANE), BF16),
                pltpu.VMEM((hd // LANE, rows, LANE), BF16),
                pltpu.VMEM((rows, LANE), F32),
                pltpu.VMEM((rows, LANE), F32),
                pltpu.VMEM((rows, LANE), jnp.int32),
                pltpu.SemaphoreType.DMA((8,)),
            ],
        ),
        out_shape=[
            jax.ShapeDtypeStruct((rows, hd + LANE), F32),
            jax.ShapeDtypeStruct(k3.shape, BF16),
            jax.ShapeDtypeStruct(v3.shape, BF16),
        ],
        compiler_params=pltpu.CompilerParams(dimension_semantics=("arbitrary",), vmem_limit_bytes=VMEM_ALL),
    )(seq_lens, seq_lens.reshape(rows // LANE, LANE), x_tok, g.reshape(1, -1), freq, k3, v3, wq, wk, wv)
    return packed, ko.reshape(k_blk.shape), vo.reshape(v_blk.shape)


def solution(mesh):
    cache_spec = P(None, "sp", "tp", None)
    col_spec = P(None, "tp")
    row_spec = P("tp", None)
    full_spec = P()

    def local_step(x_tok, seq_lens, k_blk, v_blk, g_attn, wq_loc, wk_loc, wv_loc, wo_loc, g_mlp, wg_loc, wu_loc, wd_loc):
        w = x_tok.shape[1] // NX
        res = lax.dynamic_slice(x_tok, (lax.axis_index("sp") * 8, lax.axis_index("tp") * w), (8, w)).astype(F32)
        packed, k_out, v_out = attend(x_tok, seq_lens, k_blk, v_blk, g_attn, wq_loc, wk_loc, wv_loc)
        y_out = layer(packed, res, g_mlp, wo_loc, wg_loc, wu_loc, wd_loc, x_tok.shape[0])
        return y_out, k_out, v_out

    return jax.shard_map(local_step, mesh=mesh, in_specs=(full_spec, full_spec, cache_spec, cache_spec, full_spec, col_spec, col_spec, col_spec, row_spec, full_spec, col_spec, col_spec, row_spec), out_specs=(full_spec, cache_spec, cache_spec), check_vma=False)
```

time: 460 us -> 95.9 us (0.21)
  waiting for transfers between devices: 275 us -> 0 us
  Pallas kernels: 0 us -> 87.5 us
  matrix products: 70.7 us -> 0 us
  blocking collectives: 66 us -> 0 us
  other arithmetic: 24.8 us -> 1.95 us
  between operations: 14 us -> 0.66 us
    psum x3 -> x0, waiting for transfers between devices: 275 us -> none  [the longest x1 108 us: local_step(): lax.psum(jnp.concatenate([blk_mix * factor, blk_sum * factor], axis=-1),...]
    pallas_call x0 -> x2, Pallas kernels: none -> 87.5 us  [the longest x1 71.8 us: layer(): pl.pallas_call(layer_kernel, name='layer', out_shape=jax.ShapeDtypeStruct...]
    dot_general x8 -> x0, matrix products: 70.7 us -> none  [the longest x1 31.7 us: local_step(): jnp.dot(act_prod, wd_loc, preferred_element_type=jnp.float32)]
    pmax x1 -> x0, blocking collectives: 66 us -> none  [local_step(): glob_max = lax.pmax(blk_max, 'sp')]
    reduce_sum x3 -> x0, other arithmetic: 7.27 us -> none  [the longest x2 5.38 us: rms_norm(): jnp.mean(x_f32 * x_f32, axis=-1, keepdims=True) + NORM_EPS]
    convert_element_type x5 -> x1, other arithmetic: 6.8 us -> 1.33 us  [local_step(): lax.dynamic_slice(x_tok, (lax.axis_index('sp') * 8, lax.axis_index('tp')...]
    select_n x1 -> x0, other arithmetic: 5.46 us -> none  [local_step(): v_out = jnp.where(is_new, v_new[:, None], v_blk)]
  transfers between devices with their start and end apart: 3 -> 0, of which waited for: 3 -> 0; matrix products, arithmetic and copies ran while one was open for 0% -> 0% of each run, Pallas kernels for 0% -> 0%
where the time goes in v3:
time: 95.9 us; the launch traced here: 95.5 us
  Pallas kernels  87.5 us (91%)
  local copies, waits for them, and re-layouts  5.46 us (6%)
  other arithmetic  1.95 us (2%)
    pallas_call x1, Pallas kernels, layer(): pl.pallas_call(layer_kernel, name='layer', out_shape=jax.ShapeDtypeStruct...  71.8 us
    pallas_call x1, Pallas kernels, attend(): pl.pallas_call(attend_kernel, name='attend', grid_spec=pltpu.PrefetchScal...  15.6 us
    unnamed x1, local copies, waits for them, and re-layouts  2.85 us

profile of v3, /device:TPU:1, one launch (start us, length us, event | category | flops | bytes accessed | tf_op | source)
XLA Modules:
  0.0 95.5 jit_solution(11088292919554242797)
XLA Ops:
  0.7 0.6 maximum_bitcast_fusion.freq_ref
  1.3 1.3 %reshape.34.g_ref = bf16[1,3584]{1,0:T(2,128)(2,1)} reshape(bf16[3584]{0:T(1024)(128)(2,1)} %param.17) | data formatting | bytes 14336 | tf_op jit(solution)/shard_map/reshape | solution.py:492
  2.6 1.3 %reshape.39.g_ref = bf16[1,3584]{1,0:T(2,128)(2,1)} reshape(bf16[3584]{0:T(1024)(128)(2,1)} %param.22) | data formatting | bytes 14336 | tf_op jit(solution)/shard_map/reshape | solution.py:355
  3.9 1.3 %dynamic-slice_convert_fusion.res_ref = f32[8,896]{1,0:T(8,128)} fusion(bf16[256,3584]{1,0:T(8,128)(2,1)} %x_ref.1, s32[]{:T(128)S(6)} %select_n.6, s32[]{:T(128)S(6)} %select_n.7), kind=kLoop, calls=%fused_computation | loop fusion | flops 7168 | bytes 43016 | tf_op jit(solution)/shard_map/convert_element_type | solution.py:504
  5.2 15.6 %attend.1 = (f32[256,1024]{1,0:T(8,128)}, bf16[256,32,128]{2,1,0:T(8,128)(2,1)}, bf16[256,32,128]{2,1,0:T(8,128)(2,1)}) custom-call(s32[256]{0:T(256)} %lens_ref.1, s32[2,128]{1,0:T(2,128)} %bitcast.15, bf16[256,3584]{1,0:T(8,128)(2,1)} %x_ref.1, bf16[1,3584]{1,0:T(2,128)(2,1)} %reshape.34.g_ref, f32[1,128]{1,0:T(1,128)} %maximum_bitcast_fusion.freq_ref, ...), custom_call_target="tpu_custom_call" | custom-call | tf_op jit(solution)/shard_map/attend/pallas_call | solution.py:469
  20.8 71.8 %layer.1 = bf16[256,3584]{1,0:T(8,128)(2,1)} custom-call(f32[16,2,8,1024]{3,2,1,0:T(8,128)} %bitcast.14, f32[8,896]{1,0:T(8,128)} %dynamic-slice_convert_fusion.res_ref, bf16[1,3584]{1,0:T(2,128)(2,1)} %reshape.39.g_ref, bf16[896,3584]{1,0:T(8,128)(2,1)} %wo_hbm.1, bf16[3584,4736]{1,0:T(8,128)(2,1)} %wg_hbm.1, bf16[3584,4736]{1,0:T(8,128)(2,1)} %wu_hbm.1, ...), custom_call_target="tpu_custom_call" | custom-call | tf_op jit(solution)/shard_map/layer/pallas_call | solution.py:327
  92.7 2.8 %copy.19 = bf16[256,3584]{1,0:T(8,128)(2,1)} copy(bf16[256,3584]{1,0:T(8,128)(2,1)} %layer.1) | data formatting | bytes 3670016
  (1 shorter events, 0.0 us)

commit v4 on v3

--- a/solution.py
+++ b/solution.py
@@ -1,7 +1,6 @@
-import functools
-
 import jax
 import jax.numpy as jnp
+import numpy as np
 from jax import lax
 from jax.experimental import pallas as pl
 from jax.experimental.pallas import tpu as pltpu
@@ -48,10 +47,10 @@
 
 
 def layer_kernel(
-    in_ref, res_ref, g_ref, wo_hbm, wg_hbm, wu_hbm, wd_hbm, out_ref,
-    swap, merged, slots, part, xslots, chunk, hid, hn, acc, cslot, buf,
-    wg, wu, wg_t, wu_t, wd,
-    w_sem, swap_sem, rs_send, rs_recv, xs_send, xs_recv, ag_send, ag_recv, fw_send, fw_recv,
+    q_ref, pos_ref, g_ref, x_hbm, k_hbm, v_hbm, wo_hbm, wg_hbm, wu_hbm, wd_hbm, out_ref,
+    kv, res, pack, swap, merged, slots, part, xslots, chunk, hid, hn, acc, cslot, buf,
+    wg, wu, wd,
+    w_sem, in_sem, gv_send, gv_recv, rs_send, rs_recv, xs_send, xs_recv, ag_send, ag_recv, fw_send, fw_recv,
     c_sem, xo_send, xo_recv, p1_send, p1_recv, p2_send, p2_recv, cc_send, cc_recv,
 ):
     x, z, y, c = coords()
@@ -79,6 +78,7 @@
         here = pl.ds(pl.multiple_of(i * WIN, LANE), WIN)
         return pltpu.make_async_copy(wd_hbm.at[rows, :], wd.at[here, :], w_sem.at[2, i])
 
+    wg_t, wu_t = kv.at[0, :wg.shape[1], :], kv.at[1, :wu.shape[1], :]
     tail = pl.ds(pl.multiple_of(first + wide, LANE), LANE)
     tails = (
         pltpu.make_async_copy(wg_hbm.at[:, tail], wg_t, w_sem.at[0, steps]),
@@ -88,6 +88,15 @@
     get_wo = pltpu.make_async_copy(wo_hbm, wd.at[keep:, :], w_sem.at[3, 0])
     n_keep = keep // WIN
 
+    at_me = lax.axis_index("sp")
+    get_in = [
+        pltpu.make_async_copy(k_hbm, kv.at[0], in_sem.at[0]),
+        pltpu.make_async_copy(v_hbm, kv.at[1], in_sem.at[1]),
+        pltpu.make_async_copy(x_hbm.at[pl.ds(pl.multiple_of(at_me * 8, 8), 8), pl.ds(pl.multiple_of(x * w, LANE), w)], res, in_sem.at[2]),
+        get_wo,
+    ]
+    for copy in get_in:
+        copy.start()
     planes = [
         [(turn(x, a, NX), z, turn(y, b, NY)) for a, b in XY],
         [(x, turn(z, a, NZ), turn(y, b, NY)) for a, b in XY],
@@ -97,33 +106,90 @@
     near += [(turn(x, a, NX), turn(z, b, NZ), y) for a in range(1, NX) for b in range(1, NZ)]
     entry_barrier([dev(*p, c) for p in near] + [partner])
 
-    give = remote(in_ref.at[:, mate], swap, swap_sem.at[0], swap_sem.at[1], partner)
-    give.start()
-    get_wo.start()
-    give.wait_recv()
+    n_grp = NZ * NY
+    seq = kv.shape[1] // q_ref.shape[1]
+    span = GRP * seq
     low = lax.broadcasted_iota(jnp.int32, (8, LANE), 1) < half
 
-    def pair(g):
-        s1, s2 = in_ref[g, c, :, w:], swap[g, :, w:]
+    def place(k):
+        return turn(z, ((k + 1) // NY) % NZ, NZ), turn(y, (k + 1) % NY, NY)
+
+    def give(k):
+        return remote(pack.at[k, mate], swap.at[k], gv_send.at[k], gv_recv.at[k], partner)
+
+    def deliver(k):
+        pz, py = place(k)
+        return remote(merged.at[k], slots.at[k], rs_send.at[k], rs_recv.at[k], dev(x, pz, py, c))
+
+    def attend(k):
+        pz, py = place(k)
+        g = pz * NY + py
+        at = pl.ds(pl.multiple_of(g * GRP, GRP), GRP)
+        keys = pl.ds(pl.multiple_of(g * span, span), span)
+        qs = jnp.concatenate([q_ref[h, at, :] for h in range(heads)], axis=0)
+        col = lax.broadcasted_iota(jnp.int32, (GRP, span), 1)
+        own = (col // seq) == lax.broadcasted_iota(jnp.int32, (GRP, span), 0)
+        p = jnp.concatenate([pos_ref[at, :]] * (span // LANE), axis=1)
+        valid = own & (at_me * seq + col % seq <= p)
+        valid = jnp.concatenate([valid.astype(F32)] * heads, axis=0) > 0.5
+        scores = lax.dot_general(qs, kv[0, keys, :], (((1,), (1,)), ((), ())), preferred_element_type=F32) * (LANE ** -0.5)
+        scores = jnp.where(valid, scores, -1e30)
+        top = jnp.max(scores, axis=1, keepdims=True)
+        wt = jnp.where(valid, jnp.exp(scores - top), 0.0)
+        tot = jnp.sum(wt, axis=1, keepdims=True)
+        mix = jnp.dot(wt.astype(BF16), kv[1, keys, :], preferred_element_type=F32)
+        lane = lax.broadcasted_iota(jnp.int32, (8, LANE), 1)
+        for e in range(NC):
+            stats = jnp.zeros((8, LANE), F32)
+            for h in range(heads):
+                rows = slice(h * GRP + e * 8, h * GRP + e * 8 + 8)
+                pack[k, e, :, h * LANE:(h + 1) * LANE] = mix[rows]
+                stats = jnp.where(lane == h, top[rows], stats)
+                stats = jnp.where(lane == half + h, tot[rows], stats)
+            pack[k, e, :, w:] = stats
+        give(k).start()
+
+    def pair(k):
+        give(k).wait_recv()
+        s1, s2 = pack[k, c, :, w:], swap[k, :, w:]
         top = jnp.maximum(s1, s2)
         f1, f2 = jnp.exp(s1 - top), jnp.exp(s2 - top)
         total = pltpu.roll(f1, half, 1) * s1 + pltpu.roll(f2, half, 1) * s2
         mix = []
         for h in range(heads):
             cut = slice(h * LANE, (h + 1) * LANE)
-            mix.append(f1[:, h:h + 1] * in_ref[g, c, :, cut] + f2[:, h:h + 1] * swap[g, :, cut])
+            mix.append(f1[:, h:h + 1] * pack[k, c, :, cut] + f2[:, h:h + 1] * swap[k, :, cut])
         return mix, jnp.where(low, top, total)
 
-    rs = []
-    for k, (_, pz, py) in enumerate(planes[1]):
-        g = pz * NY + py
-        mix, stats = pair(g)
+    def pass_on(k):
+        mix, stats = pair(k)
         for h in range(heads):
             merged[k, :, h * LANE:(h + 1) * LANE] = mix[h]
         merged[k, :, w:] = stats
-        copy = remote(merged.at[k], slots.at[k], rs_send.at[k], rs_recv.at[k], dev(x, pz, py, c))
-        copy.start()
-        rs.append(copy)
+        deliver(k).start()
+
+    lag = 4
+    for copy in get_in[:2]:
+        copy.wait()
+
+    def begin(k, carry):
+        attend(k)
+        return carry
+
+    def both(k, carry):
+        attend(k)
+        pass_on(k - lag)
+        return carry
+
+    def finish(k, carry):
+        pass_on(k)
+        return carry
+
+    lax.fori_loop(0, lag, begin, 0)
+    lax.fori_loop(lag, n_grp, both, 0)
+    lax.fori_loop(n_grp - lag, n_grp - 1, finish, 0)
+    rs = [deliver(k) for k in range(n_grp - 1)]
+    gives = [give(k) for k in range(n_grp)]
     for i in range(n_keep):
         for copy in fetch(i) + (fetch_down(i),):
             copy.start()
@@ -132,7 +198,7 @@
             copy.start()
     for copy in tails[:2]:
         copy.start()
-    own_mix, own_stats = pair(z * NY + y)
+    own_mix, own_stats = pair(n_grp - 1)
     for copy in rs:
         copy.wait_recv()
     top = own_stats
@@ -169,7 +235,8 @@
     for k, copy in enumerate(xs):
         copy.wait_recv()
         sums = sums + xslots[k]
-    hidden = (res_ref[...] + sums).astype(BF16).astype(F32)
+    get_in[2].wait()
+    hidden = (res[...].astype(F32) + sums).astype(BF16).astype(F32)
     chunk[...] = hidden
     ag = []
     for k, px in enumerate(line):
@@ -312,14 +379,14 @@
                 r = ((a * NY + b) * NC + e) * 8
                 for d in range(NX):
                     out_ref[r:r + 8, d * w:(d + 1) * w] = buf[a, b, e, d].astype(BF16)
-    for copy in [give, back] + rs + fw[1:] + xo + p1 + done:
+    for copy in gives + [back] + rs + fw[1:] + xo + p1 + done:
         copy.wait_send()
 
 
-def layer(packed, res, g, wo, wg, wu, wd, rows):
-    packed = packed.reshape(NZ * NY, NC, 8, packed.shape[1])
-    width = wo.shape[1]
+def layer(q, pos, x_tok, ko, vo, g, wo, wg, wu, wd):
+    rows, width = x_tok.shape
     w = width // NX
+    keys = rows * ko.shape[1]
     steps = ((wg.shape[1] // LANE + 1) // 2 * LANE) // WIN
     sem = pltpu.SemaphoreType.DMA
     vmem = pl.BlockSpec(memory_space=pltpu.VMEM)
@@ -328,12 +395,15 @@
         layer_kernel,
         name="layer",
         out_shape=jax.ShapeDtypeStruct((rows, width), BF16),
-        in_specs=[vmem] * 3 + [hbm] * 4,
+        in_specs=[vmem] * 3 + [hbm] * 7,
         out_specs=vmem,
         scratch_shapes=[
-            pltpu.VMEM((NZ * NY, 8, packed.shape[3]), F32),
-            pltpu.VMEM((15, 8, packed.shape[3]), F32),
-            pltpu.VMEM((15, 8, packed.shape[3]), F32),
+            pltpu.VMEM((2, keys, LANE), BF16),
+            pltpu.VMEM((8, w), BF16),
+            pltpu.VMEM((NZ * NY, NC, 8, w + LANE), F32),
+            pltpu.VMEM((NZ * NY, 8, w + LANE), F32),
+            pltpu.VMEM((15, 8, w + LANE), F32),
+            pltpu.VMEM((15, 8, w + LANE), F32),
             pltpu.VMEM((8, width), F32),
             pltpu.VMEM((6, 8, w), F32),
             pltpu.VMEM((8, w), F32),
@@ -344,153 +414,137 @@
             pltpu.VMEM((NZ, NY, NC, NX, 8, w), F32),
             pltpu.VMEM((steps, width, WIN), BF16),
             pltpu.VMEM((steps, width, WIN), BF16),
-            pltpu.VMEM((width, LANE), BF16),
-            pltpu.VMEM((width, LANE), BF16),
             pltpu.VMEM((steps * WIN + LANE, width), BF16),
             sem((4, steps + 1)),
-            sem((2,)), sem((15,)), sem((15,)), sem((3,)), sem((3,)), sem((3,)), sem((3,)), sem((4,)), sem((4,)),
+            sem((3,)), sem((16,)), sem((16,)), sem((15,)), sem((15,)), sem((3,)), sem((3,)), sem((3,)), sem((3,)), sem((4,)), sem((4,)),
             sem((2,)), sem((3,)), sem((3,)), sem((3, 15)), sem((3, 15)), sem((3, 6)), sem((3, 6)), sem((3, 8)), sem((3, 8)),
         ],
         compiler_params=pltpu.CompilerParams(collective_id=0, has_side_effects=True, vmem_limit_bytes=VMEM_ALL),
-    )(packed, res, g.reshape(1, -1), wo, wg, wu, wd)
+    )(q, pos, g, x_tok, ko.reshape(keys, LANE), vo.reshape(keys, LANE), wo, wg, wu, wd)
 
 
 GRP = 16
-SUB = 4
-
-
-def attend_kernel(lens_ref, lens_row, x_ref, g_ref, freq_ref, k_ref, v_ref, wq_hbm, wk_hbm, wv_hbm, pack_ref, ko_ref, vo_ref, w, q, knew, vnew, pos, sem):
-    step = pl.program_id(0)
-    rows = x_ref.shape[0]
-    heads = wq_hbm.shape[1] // LANE
-    seq = k_ref.shape[1]
+
+
+def project_kernel(lens_ref, lens_row, g_ref, freq_ref, x_hbm, k_hbm, v_hbm, wq_hbm, wk_hbm, wv_hbm, q_ref, pos_ref, ko_hbm, vo_hbm, xs, u, w, kv, knew, vnew, sem, out_sem):
+    rows, width = xs.shape
+    heads = q_ref.shape[0]
+    hd = heads * LANE
+    seq = kv.shape[2]
     half = LANE // 2
-    hd = heads * LANE
     base = lax.axis_index("sp") * seq
-
-    @pl.when(step == 0)
-    def project():
-        odd = hd % (2 * LANE)
-        cuts = [(i, 2 * LANE) for i in range(0, hd - odd, 2 * LANE)]
-        copies = [[pltpu.make_async_copy(wq_hbm.at[:, a:a + n], w.at[:, a:a + n], sem.at[i])] for i, (a, n) in enumerate(cuts)]
-        n = len(cuts)
-        last = [
-            pltpu.make_async_copy(wq_hbm.at[:, hd - odd:], w.at[:, hd - odd:hd], sem.at[n]),
-            pltpu.make_async_copy(wk_hbm, w.at[:, hd:hd + LANE], sem.at[n + 1]),
-        ]
-        copies += [last, [pltpu.make_async_copy(wv_hbm, w.at[:, hd + LANE:], sem.at[n + 2])]]
-        cuts += [(hd - odd, odd + LANE), (hd + LANE, LANE)]
-        for group in copies:
-            for copy in group:
-                copy.start()
-        x32 = x_ref[...].astype(F32)
+    n_x, n_out = 2, 4
+    part = rows // n_x
+    get_x = [pltpu.make_async_copy(x_hbm.at[i * part:(i + 1) * part], xs.at[i * part:(i + 1) * part], sem.at[i]) for i in range(n_x)]
+    get_kv = [
+        pltpu.make_async_copy(wk_hbm, w.at[:, hd:hd + LANE], sem.at[2]),
+        pltpu.make_async_copy(wv_hbm, w.at[:, hd + LANE:], sem.at[3]),
+    ]
+    get_cache = [pltpu.make_async_copy(k_hbm, kv.at[0], sem.at[4]), pltpu.make_async_copy(v_hbm, kv.at[1], sem.at[5])]
+    cuts = [(i, min(2 * LANE, hd - i)) for i in range(0, hd, 2 * LANE)]
+    get_q = [pltpu.make_async_copy(wq_hbm.at[:, i:i + n], w.at[:, i:i + n], sem.at[6 + j]) for j, (i, n) in enumerate(cuts)]
+    for copy in get_x + get_kv + get_cache + get_q:
+        copy.start()
+
+    eye = lax.broadcasted_iota(jnp.int32, (LANE, LANE), 0) == lax.broadcasted_iota(jnp.int32, (LANE, LANE), 1)
+    cols = []
+    for i in range(rows // LANE):
+        line = lens_row[i:i + 1, :].astype(F32)
+        col = jnp.sum(jnp.where(eye, line, 0.0), axis=1, keepdims=True)
+        pos_ref[i * LANE:(i + 1) * LANE, :] = jnp.broadcast_to(col, (LANE, LANE)).astype(jnp.int32)
+        cols.append(col)
+    low = lax.broadcasted_iota(jnp.int32, (LANE, LANE), 1) < half
+    angles = jnp.where(low, cols[0], cols[1]) * freq_ref[...]
+    cos = jnp.cos(angles)
+    sin = jnp.sin(angles)
+    cos_r = pltpu.roll(cos, half, 1)
+    sin_r = pltpu.roll(sin, half, 1)
+    cos_t = jnp.concatenate([jnp.where(low, cos, cos_r), jnp.where(low, cos_r, cos)], axis=0)
+    sin_t = jnp.concatenate([jnp.where(low, -sin, sin_r), jnp.where(low, -sin_r, sin)], axis=0)
+
+    def norm(i, carry):
+        at = pl.ds(pl.multiple_of(i * GRP, GRP), GRP)
+        x32 = xs[at, :].astype(F32)
         inv = lax.rsqrt(jnp.mean(x32 * x32, axis=-1, keepdims=True) + NORM_EPS)
-        u = (x32 * inv * g_ref[...].astype(F32)).astype(BF16)
-        eye = lax.broadcasted_iota(jnp.int32, (LANE, LANE), 0) == lax.broadcasted_iota(jnp.int32, (LANE, LANE), 1)
-        cols = []
-        for i in range(rows // LANE):
-            line = lens_row[i:i + 1, :].astype(F32)
-            col = jnp.sum(jnp.where(eye, line, 0.0), axis=1, keepdims=True)
-            pos[i * LANE:(i + 1) * LANE, :] = jnp.broadcast_to(col, (LANE, LANE)).astype(jnp.int32)
-            cols.append(col)
-        low = lax.broadcasted_iota(jnp.int32, (LANE, LANE), 1) < half
-        angles = jnp.where(low, cols[0], cols[1]) * freq_ref[...]
-        cos = jnp.cos(angles)
-        sin = jnp.sin(angles)
-        cos_r = pltpu.roll(cos, half, 1)
-        sin_r = pltpu.roll(sin, half, 1)
-        cos_t = jnp.concatenate([jnp.where(low, cos, cos_r), jnp.where(low, cos_r, cos)], axis=0)
-        sin_t = jnp.concatenate([jnp.where(low, -sin, sin_r), jnp.where(low, -sin_r, sin)], axis=0)
-        for group, (a, n) in zip(copies, cuts):
-            for copy in group:
-                copy.wait()
-            out = jnp.dot(u, w[:, a:a + n], preferred_element_type=F32).astype(BF16).astype(F32)
-            for j in range(0, n, LANE):
-                h = (a + j) // LANE
-                part = out[:, j:j + LANE]
-                if h <= heads:
-                    part = (part * cos_t + pltpu.roll(part, half, 1) * sin_t).astype(BF16)
-                if h < heads:
-                    q[h] = part
-                elif h == heads:
-                    knew[...] = part.astype(F32)
-                else:
-                    vnew[...] = part
-
-    first = step * SUB * GRP
+        u[at, :] = (x32 * inv * g_ref[...].astype(F32)).astype(BF16)
+        return carry
+
+    for i in range(n_x):
+        get_x[i].wait()
+        lax.fori_loop(i * part // GRP, (i + 1) * part // GRP, norm, 0)
+
+    def rope(t):
+        return (t * cos_t + pltpu.roll(t, half, 1) * sin_t).astype(BF16)
+
+    for copy in get_kv:
+        copy.wait()
+    out = jnp.dot(u[...], w[:, hd:], preferred_element_type=F32).astype(BF16).astype(F32)
+    knew[...] = rope(out[:, :LANE]).astype(F32)
+    vnew[...] = out[:, LANE:]
+    for copy in get_cache:
+        copy.wait()
     line = lax.broadcasted_iota(jnp.int32, (seq, LANE), 0)
-    for b in range(SUB * GRP):
-        here = line == lens_ref[first + b] - base
-        k_row = knew[pl.ds(first + b, 1), :]
-        v_row = vnew[pl.ds(first + b, 1), :]
-        ko_ref[b] = jnp.where(here, k_row, k_ref[b].astype(F32)).astype(BF16)
-        vo_ref[b] = jnp.where(here, v_row, v_ref[b].astype(F32)).astype(BF16)
-    span = GRP * seq
-    col = lax.broadcasted_iota(jnp.int32, (GRP, span), 1)
-    own = (col // seq) == lax.broadcasted_iota(jnp.int32, (GRP, span), 0)
-    where_at = base + col % seq
-    lane = lax.broadcasted_iota(jnp.int32, (GRP, LANE), 1)
-    for s in range(SUB):
-        at = pl.ds(pl.multiple_of(first + s * GRP, GRP), GRP)
-        block = slice(s * GRP, (s + 1) * GRP)
-        qs = jnp.concatenate([q[h, at, :] for h in range(heads)], axis=0)
-        ks = ko_ref[block].reshape(span, LANE)
-        vs = vo_ref[block].reshape(span, LANE)
-        p = jnp.concatenate([pos[at, :]] * (span // LANE), axis=1)
-        valid = own & (where_at <= p)
-        valid = jnp.concatenate([valid.astype(F32)] * heads, axis=0) > 0.5
-        scores = lax.dot_general(qs, ks, (((1,), (1,)), ((), ())), preferred_element_type=F32) * (LANE ** -0.5)
-        scores = jnp.where(valid, scores, -1e30)
-        top = jnp.max(scores, axis=1, keepdims=True)
-        wt = jnp.where(valid, jnp.exp(scores - top), 0.0)
-        tot = jnp.sum(wt, axis=1, keepdims=True)
-        mix = jnp.dot(wt.astype(BF16), vs, preferred_element_type=F32)
-        stats = jnp.zeros((GRP, LANE), F32)
-        for h in range(heads):
-            part = slice(h * GRP, (h + 1) * GRP)
-            pack_ref[block, h * LANE:(h + 1) * LANE] = mix[part]
-            stats = jnp.where(lane == h, top[part], stats)
-            stats = jnp.where(lane == half + h, tot[part], stats)
-        pack_ref[block, hd:] = stats
-
-
-def attend(x_tok, seq_lens, k_blk, v_blk, g, wq, wk, wv):
+
+    def put(i, carry):
+        for j in range(GRP):
+            b = i * GRP + j
+            here = line == lens_ref[b] - base
+            kv[0, b] = jnp.where(here, knew[pl.ds(b, 1), :], kv[0, b].astype(F32)).astype(BF16)
+            kv[1, b] = jnp.where(here, vnew[pl.ds(b, 1), :], kv[1, b].astype(F32)).astype(BF16)
+        return carry
+
+    puts = []
+    part = rows // n_out
+    for i in range(n_out):
+        lax.fori_loop(i * part // GRP, (i + 1) * part // GRP, put, 0)
+        at = slice(i * part, (i + 1) * part)
+        for j, ref in enumerate((ko_hbm, vo_hbm)):
+            copy = pltpu.make_async_copy(kv.at[j, at], ref.at[at], out_sem.at[j, i])
+            copy.start()
+            puts.append(copy)
+    for copy, (a, n) in zip(get_q, cuts):
+        copy.wait()
+        out = jnp.dot(u[...], w[:, a:a + n], preferred_element_type=F32).astype(BF16).astype(F32)
+        for j in range(0, n, LANE):
+            q_ref[(a + j) // LANE] = rope(out[:, j:j + LANE])
+    for copy in puts:
+        copy.wait()
+
+
+def project(x_tok, seq_lens, k_blk, v_blk, g, wq, wk, wv):
     rows, width = x_tok.shape
     seq = k_blk.shape[1]
     hd = wq.shape[1]
     half = LANE // 2
-    freq = jnp.power(F32(ROPE_BASE), jnp.arange(half, dtype=F32) * (-2.0 / LANE))
-    freq = jnp.concatenate([freq, freq]).reshape(1, LANE)
-    step = SUB * GRP
-    whole = lambda shape: pl.BlockSpec(shape, lambda i, *_: (0,) * len(shape))
-    cache = pl.BlockSpec((step, seq, LANE), lambda i, *_: (i, 0, 0))
+    freq = np.float32(ROPE_BASE) ** (np.arange(half, dtype=np.float32) * np.float32(-2.0 / LANE))
+    freq = jnp.asarray(np.concatenate([freq, freq]).reshape(1, LANE).astype(np.float32))
+    vmem = pl.BlockSpec(memory_space=pltpu.VMEM)
     hbm = pl.BlockSpec(memory_space=pl.ANY)
-    k3, v3 = k_blk.reshape(rows, seq, LANE), v_blk.reshape(rows, seq, LANE)
-    packed, ko, vo = pl.pallas_call(
-        attend_kernel,
-        name="attend",
-        grid_spec=pltpu.PrefetchScalarGridSpec(
-            num_scalar_prefetch=1,
-            grid=(rows // step,),
-            in_specs=[whole((rows // LANE, LANE)), whole((rows, width)), whole((1, width)), whole((1, LANE)), cache, cache, hbm, hbm, hbm],
-            out_specs=[pl.BlockSpec((step, hd + LANE), lambda i, *_: (i, 0)), cache, cache],
-            scratch_shapes=[
-                pltpu.VMEM((width, hd + 2 * LANE), BF16),
-                pltpu.VMEM((hd // LANE, rows, LANE), BF16),
-                pltpu.VMEM((rows, LANE), F32),
-                pltpu.VMEM((rows, LANE), F32),
-                pltpu.VMEM((rows, LANE), jnp.int32),
-                pltpu.SemaphoreType.DMA((8,)),
-            ],
-        ),
+    sem = pltpu.SemaphoreType.DMA
+    cache = jax.ShapeDtypeStruct((rows, seq, LANE), BF16)
+    return pl.pallas_call(
+        project_kernel,
+        name="project",
         out_shape=[
-            jax.ShapeDtypeStruct((rows, hd + LANE), F32),
-            jax.ShapeDtypeStruct(k3.shape, BF16),
-            jax.ShapeDtypeStruct(v3.shape, BF16),
+            jax.ShapeDtypeStruct((hd // LANE, rows, LANE), BF16),
+            jax.ShapeDtypeStruct((rows, LANE), jnp.int32),
+            cache,
+            cache,
         ],
-        compiler_params=pltpu.CompilerParams(dimension_semantics=("arbitrary",), vmem_limit_bytes=VMEM_ALL),
-    )(seq_lens, seq_lens.reshape(rows // LANE, LANE), x_tok, g.reshape(1, -1), freq, k3, v3, wq, wk, wv)
-    return packed, ko.reshape(k_blk.shape), vo.reshape(v_blk.shape)
+        in_specs=[pl.BlockSpec(memory_space=pltpu.SMEM), vmem, vmem, vmem] + [hbm] * 6,
+        out_specs=[vmem, vmem, hbm, hbm],
+        scratch_shapes=[
+            pltpu.VMEM((rows, width), BF16),
+            pltpu.VMEM((rows, width), BF16),
+            pltpu.VMEM((width, hd + 2 * LANE), BF16),
+            pltpu.VMEM((2, rows, seq, LANE), BF16),
+            pltpu.VMEM((rows, LANE), F32),
+            pltpu.VMEM((rows, LANE), F32),
+            sem((10,)),
+            sem((2, 4)),
+        ],
+        compiler_params=pltpu.CompilerParams(vmem_limit_bytes=VMEM_ALL),
+    )(seq_lens, seq_lens.reshape(rows // LANE, LANE), g, freq, x_tok, k_blk.reshape(cache.shape), v_blk.reshape(cache.shape), wq, wk, wv)
 
 
 def solution(mesh):
@@ -500,10 +554,8 @@
     full_spec = P()
 
     def local_step(x_tok, seq_lens, k_blk, v_blk, g_attn, wq_loc, wk_loc, wv_loc, wo_loc, g_mlp, wg_loc, wu_loc, wd_loc):
-        w = x_tok.shape[1] // NX
-        res = lax.dynamic_slice(x_tok, (lax.axis_index("sp") * 8, lax.axis_index("tp") * w), (8, w)).astype(F32)
-        packed, k_out, v_out = attend(x_tok, seq_lens, k_blk, v_blk, g_attn, wq_loc, wk_loc, wv_loc)
-        y_out = layer(packed, res, g_mlp, wo_loc, wg_loc, wu_loc, wd_loc, x_tok.shape[0])
-        return y_out, k_out, v_out
+        q, pos, ko, vo = project(x_tok, seq_lens, k_blk, v_blk, g_attn, wq_loc, wk_loc, wv_loc)
+        y_out = layer(q, pos, x_tok, ko, vo, g_mlp, wo_loc, wg_loc, wu_loc, wd_loc)
+        return y_out, ko.reshape(k_blk.shape), vo.reshape(v_blk.shape)
 
     return jax.shard_map(local_step, mesh=mesh, in_specs=(full_spec, full_spec, cache_spec, cache_spec, full_spec, col_spec, col_spec, col_spec, row_spec, full_spec, col_spec, col_spec, row_spec), out_specs=(full_spec, cache_spec, cache_spec), check_vma=False)

time: 95.9 us -> 89.4 us (0.932)
  local copies, waits for them, and re-layouts: 5.46 us -> 2.85 us
  other arithmetic: 1.95 us -> 0 us
  Pallas kernels: 87.5 us -> 85.7 us
    pallas_call x1, Pallas kernels: 15.6 us -> 11.6 us  [project(): pl.pallas_call(project_kernel, name='project', out_shape=[jax.ShapeDtypeS...]
    reshape x2 -> x0, local copies, waits for them, and re-layouts: 2.61 us -> none  [the longest x1 1.3 us: layer(): g.reshape(1, -1)]
    pallas_call x1, Pallas kernels: 71.8 us -> 74.1 us  [layer(): pl.pallas_call(layer_kernel, name='layer', out_shape=jax.ShapeDtypeStruct...]
    convert_element_type x1 -> x0, other arithmetic: 1.33 us -> none  [local_step(): lax.dynamic_slice(x_tok, (lax.axis_index('sp') * 8, lax.axis_index('tp')...]
where the time goes in v4:
time: 89.4 us; the launch traced here: 89.2 us
  Pallas kernels  85.7 us (96%)
  local copies, waits for them, and re-layouts  2.85 us (3%)
    pallas_call x1, Pallas kernels, layer(): pl.pallas_call(layer_kernel, name='layer', out_shape=jax.ShapeDtypeStruct...  74.1 us
    pallas_call x1, Pallas kernels, project(): pl.pallas_call(project_kernel, name='project', out_shape=[jax.ShapeDtypeS...  11.6 us
    unnamed x1, local copies, waits for them, and re-layouts  2.85 us

profile of v4, /device:TPU:1, one launch (start us, length us, event | category | flops | bytes accessed | tf_op | source)
XLA Modules:
  0.0 89.2 jit_solution(15407077420087252953)
XLA Ops:
  0.6 11.6 %project.1 = (bf16[7,256,128]{2,1,0:T(8,128)(2,1)}, s32[256,128]{1,0:T(8,128)}, bf16[256,32,128]{2,1,0:T(8,128)(2,1)}, bf16[256,32,128]{2,1,0:T(8,128)(2,1)}) custom-call(s32[256]{0:T(256)} %lens_ref.1, s32[2,128]{1,0:T(2,128)} %bitcast.17, bf16[3584]{0:T(1024)(128)(2,1)} %g_ref.2, f32[1,128]{1,0:T(1,128)} %constant.2.clone.freq_ref, ...), custom_call_target="tpu_custom_call" | custom-call | tf_op jit(solution)/shard_map/project/pallas_call | solution.py:525
  12.2 74.1 %layer.1 = bf16[256,3584]{1,0:T(8,128)(2,1)} custom-call(bf16[7,256,128]{2,1,0:T(8,128)(2,1)} %get-tuple-element.7.q_ref, s32[256,128]{1,0:T(8,128)} %get-tuple-element.8.pos_ref, bf16[3584]{0:T(1024)(128)(2,1)} %g_ref.3, bf16[256,3584]{1,0:T(8,128)(2,1)} %x_hbm.3, bf16[8192,128]{1,0:T(8,128)(2,1)} %bitcast.11, bf16[8192,128]{1,0:T(8,128)(2,1)} %bitcast.13, ...), custom_call_target="tpu_custom_call" | custom-call | tf_op jit(solution)/shard_map/layer/pallas_call | solution.py:394
  86.4 2.8 %copy.20 = bf16[256,3584]{1,0:T(8,128)(2,1)} copy(bf16[256,3584]{1,0:T(8,128)(2,1)} %layer.1) | data formatting | bytes 3670016

commit v5 on v4

--- a/solution.py
+++ b/solution.py
@@ -47,10 +47,10 @@
 
 
 def layer_kernel(
-    q_ref, pos_ref, g_ref, x_hbm, k_hbm, v_hbm, wo_hbm, wg_hbm, wu_hbm, wd_hbm, out_ref,
-    kv, res, pack, swap, merged, slots, part, xslots, chunk, hid, hn, acc, cslot, buf,
+    q_hbm, pos_hbm, g_hbm, x_hbm, k_hbm, v_hbm, wo_hbm, wg_hbm, wu_hbm, wd_hbm, out_hbm,
+    q_ref, pos_ref, g_ref, kv, res, pack, swap, merged, slots, part, xslots, chunk, hid, hn, acc, cslot, buf,
     wg, wu, wd,
-    w_sem, in_sem, gv_send, gv_recv, rs_send, rs_recv, xs_send, xs_recv, ag_send, ag_recv, fw_send, fw_recv,
+    w_sem, out_sem, in_sem, gv_send, gv_recv, rs_send, rs_recv, xs_send, xs_recv, ag_send, ag_recv, fw_send, fw_recv,
     c_sem, xo_send, xo_recv, p1_send, p1_recv, p2_send, p2_recv, cc_send, cc_recv,
 ):
     x, z, y, c = coords()
@@ -93,10 +93,13 @@
         pltpu.make_async_copy(k_hbm, kv.at[0], in_sem.at[0]),
         pltpu.make_async_copy(v_hbm, kv.at[1], in_sem.at[1]),
         pltpu.make_async_copy(x_hbm.at[pl.ds(pl.multiple_of(at_me * 8, 8), 8), pl.ds(pl.multiple_of(x * w, LANE), w)], res, in_sem.at[2]),
-        get_wo,
+        pltpu.make_async_copy(q_hbm, q_ref, in_sem.at[3]),
+        pltpu.make_async_copy(pos_hbm, pos_ref, in_sem.at[4]),
+        pltpu.make_async_copy(g_hbm, g_ref, in_sem.at[5]),
     ]
-    for copy in get_in:
-        copy.start()
+    for copy in (get_in[3], get_in[4], get_in[0], get_in[1], get_in[2], get_in[5]):
+        copy.start()
+    fetch(0)[0].start()
     planes = [
         [(turn(x, a, NX), z, turn(y, b, NY)) for a, b in XY],
         [(x, turn(z, a, NZ), turn(y, b, NY)) for a, b in XY],
@@ -169,16 +172,18 @@
         deliver(k).start()
 
     lag = 4
-    for copy in get_in[:2]:
-        copy.wait()
+    for i in (0, 1, 3, 4):
+        get_in[i].wait()
 
     def begin(k, carry):
         attend(k)
         return carry
 
     def both(k, carry):
-        attend(k)
-        pass_on(k - lag)
+        for j in (2 * k, 2 * k + 1):
+            attend(j)
+            pass_on(j - lag)
+        fetch(k - lag // 2 + 1)[0].start()
         return carry
 
     def finish(k, carry):
@@ -186,18 +191,17 @@
         return carry
 
     lax.fori_loop(0, lag, begin, 0)
-    lax.fori_loop(lag, n_grp, both, 0)
+    lax.fori_loop(lag // 2, n_grp // 2, both, 0)
     lax.fori_loop(n_grp - lag, n_grp - 1, finish, 0)
     rs = [deliver(k) for k in range(n_grp - 1)]
     gives = [give(k) for k in range(n_grp)]
-    for i in range(n_keep):
-        for copy in fetch(i) + (fetch_down(i),):
-            copy.start()
-    for i in range(n_keep, steps):
-        for copy in fetch(i):
-            copy.start()
-    for copy in tails[:2]:
-        copy.start()
+    early = 1 + (n_grp - lag) // 2
+    get_wo.start()
+    for i in range(steps):
+        fetch(i)[1].start()
+    for i in range(early, steps):
+        fetch(i)[0].start()
+    fetch_down(0).start()
     own_mix, own_stats = pair(n_grp - 1)
     for copy in rs:
         copy.wait_recv()
@@ -228,9 +232,8 @@
         copy = remote(part.at[:, cols[k]], xslots.at[k], xs_send.at[k], xs_recv.at[k], dev(px, z, y, c))
         copy.start()
         xs.append(copy)
-    for i in range(n_keep, steps):
+    for i in range(1, 5):
         fetch_down(i).start()
-    tails[2].start()
     sums = part[:, my_cols]
     for k, copy in enumerate(xs):
         copy.wait_recv()
@@ -246,6 +249,10 @@
     fw = [remote(chunk, hid.at[my_rows, my_cols], fw_send.at[3], fw_recv.at[3], partner)]
     fw[0].start()
     hid[my_rows, my_cols] = hidden
+    for i in range(5, steps):
+        fetch_down(i).start()
+    for copy in tails:
+        copy.start()
     for k, copy in enumerate(ag):
         copy.wait_recv()
         block = hid.at[my_rows, cols[2 - k]]
@@ -254,6 +261,8 @@
         fw.append(copy)
     for copy in fw:
         copy.wait_recv()
+
+    get_in[5].wait()
 
     h32 = hid[...]
     inv = lax.rsqrt(jnp.mean(h32 * h32, axis=-1, keepdims=True) + NORM_EPS)
@@ -373,14 +382,21 @@
         crossed += [across(p, far, 1, 7)]
     for copy in crossed:
         copy.wait_recv()
+    puts = []
     for a in range(NZ):
         for b in range(NY):
             for e in range(NC):
                 r = ((a * NY + b) * NC + e) * 8
                 for d in range(NX):
-                    out_ref[r:r + 8, d * w:(d + 1) * w] = buf[a, b, e, d].astype(BF16)
+                    wd[r:r + 8, d * w:(d + 1) * w] = buf[a, b, e, d].astype(BF16)
+        at = slice(a * NY * NC * 8, (a + 1) * NY * NC * 8)
+        put = pltpu.make_async_copy(wd.at[at, :], out_hbm.at[at, :], out_sem.at[a])
+        put.start()
+        puts.append(put)
     for copy in gives + [back] + rs + fw[1:] + xo + p1 + done:
         copy.wait_send()
+    for put in puts:
+        put.wait()
 
 
 def layer(q, pos, x_tok, ko, vo, g, wo, wg, wu, wd):
@@ -389,15 +405,17 @@
     keys = rows * ko.shape[1]
     steps = ((wg.shape[1] // LANE + 1) // 2 * LANE) // WIN
     sem = pltpu.SemaphoreType.DMA
-    vmem = pl.BlockSpec(memory_space=pltpu.VMEM)
     hbm = pl.BlockSpec(memory_space=pl.ANY)
     return pl.pallas_call(
         layer_kernel,
         name="layer",
         out_shape=jax.ShapeDtypeStruct((rows, width), BF16),
-        in_specs=[vmem] * 3 + [hbm] * 7,
-        out_specs=vmem,
+        in_specs=[hbm] * 10,
+        out_specs=hbm,
         scratch_shapes=[
+            pltpu.VMEM(q.shape, BF16),
+            pltpu.VMEM(pos.shape, jnp.int32),
+            pltpu.VMEM(g.shape, BF16),
             pltpu.VMEM((2, keys, LANE), BF16),
             pltpu.VMEM((8, w), BF16),
             pltpu.VMEM((NZ * NY, NC, 8, w + LANE), F32),
@@ -416,7 +434,8 @@
             pltpu.VMEM((steps, width, WIN), BF16),
             pltpu.VMEM((steps * WIN + LANE, width), BF16),
             sem((4, steps + 1)),
-            sem((3,)), sem((16,)), sem((16,)), sem((15,)), sem((15,)), sem((3,)), sem((3,)), sem((3,)), sem((3,)), sem((4,)), sem((4,)),
+            sem((NZ,)),
+            sem((6,)), sem((16,)), sem((16,)), sem((15,)), sem((15,)), sem((3,)), sem((3,)), sem((3,)), sem((3,)), sem((4,)), sem((4,)),
             sem((2,)), sem((3,)), sem((3,)), sem((3, 15)), sem((3, 15)), sem((3, 6)), sem((3, 6)), sem((3, 8)), sem((3, 8)),
         ],
         compiler_params=pltpu.CompilerParams(collective_id=0, has_side_effects=True, vmem_limit_bytes=VMEM_ALL),
@@ -426,7 +445,10 @@
 GRP = 16
 
 
-def project_kernel(lens_ref, lens_row, g_ref, freq_ref, x_hbm, k_hbm, v_hbm, wq_hbm, wk_hbm, wv_hbm, q_ref, pos_ref, ko_hbm, vo_hbm, xs, u, w, kv, knew, vnew, sem, out_sem):
+def project_kernel(
+    lens_hbm, line_hbm, g_hbm, freq_hbm, x_hbm, k_hbm, v_hbm, wq_hbm, wk_hbm, wv_hbm, q_hbm, pos_hbm, ko_hbm, vo_hbm,
+    lens_ref, lens_row, g_ref, freq_ref, q_ref, pos_ref, xs, u, w, kv, knew, vnew, sem, small_sem, out_sem, q_sem,
+):
     rows, width = xs.shape
     heads = q_ref.shape[0]
     hd = heads * LANE
@@ -443,8 +465,16 @@
     get_cache = [pltpu.make_async_copy(k_hbm, kv.at[0], sem.at[4]), pltpu.make_async_copy(v_hbm, kv.at[1], sem.at[5])]
     cuts = [(i, min(2 * LANE, hd - i)) for i in range(0, hd, 2 * LANE)]
     get_q = [pltpu.make_async_copy(wq_hbm.at[:, i:i + n], w.at[:, i:i + n], sem.at[6 + j]) for j, (i, n) in enumerate(cuts)]
-    for copy in get_x + get_kv + get_cache + get_q:
-        copy.start()
+    get_small = [
+        pltpu.make_async_copy(line_hbm, lens_row, small_sem.at[0]),
+        pltpu.make_async_copy(freq_hbm, freq_ref, small_sem.at[1]),
+        pltpu.make_async_copy(g_hbm, g_ref, small_sem.at[2]),
+        pltpu.make_async_copy(lens_hbm, lens_ref, small_sem.at[3]),
+    ]
+    for copy in get_small + get_x + get_kv + get_cache + get_q:
+        copy.start()
+    for copy in get_small[:3]:
+        copy.wait()
 
     eye = lax.broadcasted_iota(jnp.int32, (LANE, LANE), 0) == lax.broadcasted_iota(jnp.int32, (LANE, LANE), 1)
     cols = []
@@ -453,6 +483,8 @@
         col = jnp.sum(jnp.where(eye, line, 0.0), axis=1, keepdims=True)
         pos_ref[i * LANE:(i + 1) * LANE, :] = jnp.broadcast_to(col, (LANE, LANE)).astype(jnp.int32)
         cols.append(col)
+    puts = [pltpu.make_async_copy(pos_ref, pos_hbm, q_sem.at[len(cuts)])]
+    puts[0].start()
     low = lax.broadcasted_iota(jnp.int32, (LANE, LANE), 1) < half
     angles = jnp.where(low, cols[0], cols[1]) * freq_ref[...]
     cos = jnp.cos(angles)
@@ -481,7 +513,7 @@
     out = jnp.dot(u[...], w[:, hd:], preferred_element_type=F32).astype(BF16).astype(F32)
     knew[...] = rope(out[:, :LANE]).astype(F32)
     vnew[...] = out[:, LANE:]
-    for copy in get_cache:
+    for copy in get_cache + get_small[3:]:
         copy.wait()
     line = lax.broadcasted_iota(jnp.int32, (seq, LANE), 0)
 
@@ -493,7 +525,6 @@
             kv[1, b] = jnp.where(here, vnew[pl.ds(b, 1), :], kv[1, b].astype(F32)).astype(BF16)
         return carry
 
-    puts = []
     part = rows // n_out
     for i in range(n_out):
         lax.fori_loop(i * part // GRP, (i + 1) * part // GRP, put, 0)
@@ -502,11 +533,15 @@
             copy = pltpu.make_async_copy(kv.at[j, at], ref.at[at], out_sem.at[j, i])
             copy.start()
             puts.append(copy)
-    for copy, (a, n) in zip(get_q, cuts):
+    for i, (copy, (a, n)) in enumerate(zip(get_q, cuts)):
         copy.wait()
         out = jnp.dot(u[...], w[:, a:a + n], preferred_element_type=F32).astype(BF16).astype(F32)
         for j in range(0, n, LANE):
             q_ref[(a + j) // LANE] = rope(out[:, j:j + LANE])
+        at = slice(a // LANE, (a + n) // LANE)
+        copy = pltpu.make_async_copy(q_ref.at[at], q_hbm.at[at], q_sem.at[i])
+        copy.start()
+        puts.append(copy)
     for copy in puts:
         copy.wait()
 
@@ -518,7 +553,6 @@
     half = LANE // 2
     freq = np.float32(ROPE_BASE) ** (np.arange(half, dtype=np.float32) * np.float32(-2.0 / LANE))
     freq = jnp.asarray(np.concatenate([freq, freq]).reshape(1, LANE).astype(np.float32))
-    vmem = pl.BlockSpec(memory_space=pltpu.VMEM)
     hbm = pl.BlockSpec(memory_space=pl.ANY)
     sem = pltpu.SemaphoreType.DMA
     cache = jax.ShapeDtypeStruct((rows, seq, LANE), BF16)
@@ -531,9 +565,15 @@
             cache,
             cache,
         ],
-        in_specs=[pl.BlockSpec(memory_space=pltpu.SMEM), vmem, vmem, vmem] + [hbm] * 6,
-        out_specs=[vmem, vmem, hbm, hbm],
+        in_specs=[hbm] * 10,
+        out_specs=[hbm] * 4,
         scratch_shapes=[
+            pltpu.SMEM(seq_lens.shape, jnp.int32),
+            pltpu.VMEM((rows // LANE, LANE), jnp.int32),
+            pltpu.VMEM(g.shape, BF16),
+            pltpu.VMEM((1, LANE), F32),
+            pltpu.VMEM((hd // LANE, rows, LANE), BF16),
+            pltpu.VMEM((rows, LANE), jnp.int32),
             pltpu.VMEM((rows, width), BF16),
             pltpu.VMEM((rows, width), BF16),
             pltpu.VMEM((width, hd + 2 * LANE), BF16),
@@ -541,7 +581,9 @@
             pltpu.VMEM((rows, LANE), F32),
             pltpu.VMEM((rows, LANE), F32),
             sem((10,)),
+            sem((4,)),
             sem((2, 4)),
+            sem((6,)),
         ],
         compiler_params=pltpu.CompilerParams(vmem_limit_bytes=VMEM_ALL),
     )(seq_lens, seq_lens.reshape(rows // LANE, LANE), g, freq, x_tok, k_blk.reshape(cache.shape), v_blk.reshape(cache.shape), wq, wk, wv)

time: 89.4 us -> 91.1 us (1.019)
  Pallas kernels: 85.7 us -> 87.5 us
    pallas_call x1, Pallas kernels: 11.6 us -> 14.2 us  [project(): pl.pallas_call(project_kernel, name='project', out_shape=[jax.ShapeDtypeS...]
where the time goes in v5:
time: 91.1 us; the launch traced here: 91 us
  Pallas kernels  87.5 us (96%)
  local copies, waits for them, and re-layouts  2.85 us (3%)
    pallas_call x1, Pallas kernels, layer(): pl.pallas_call(layer_kernel, name='layer', out_shape=jax.ShapeDtypeStruct...  73.3 us
    pallas_call x1, Pallas kernels, project(): pl.pallas_call(project_kernel, name='project', out_shape=[jax.ShapeDtypeS...  14.2 us
    unnamed x1, local copies, waits for them, and re-layouts  2.85 us

profile of v5, /device:TPU:1, one launch (start us, length us, event | category | flops | bytes accessed | tf_op | source)
XLA Modules:
  0.0 91.0 jit_solution(15137278258780835696)
XLA Ops:
  0.6 14.2 %project.1 = (bf16[7,256,128]{2,1,0:T(8,128)(2,1)}, s32[256,128]{1,0:T(8,128)}, bf16[256,32,128]{2,1,0:T(8,128)(2,1)}, bf16[256,32,128]{2,1,0:T(8,128)(2,1)}) custom-call(s32[256]{0:T(256)} %lens_hbm.1, s32[2,128]{1,0:T(2,128)} %bitcast.17, bf16[3584]{0:T(1024)(128)(2,1)} %g_hbm.2, f32[1,128]{1,0:T(1,128)} %constant.2.clone.freq_hbm, ...), custom_call_target="tpu_custom_call" | custom-call | tf_op jit(solution)/shard_map/project/pallas_call | solution.py:559
  14.8 73.3 %layer.1 = bf16[256,3584]{1,0:T(8,128)(2,1)} custom-call(bf16[7,256,128]{2,1,0:T(8,128)(2,1)} %get-tuple-element.7.q_hbm, s32[256,128]{1,0:T(8,128)} %get-tuple-element.8.pos_hbm, bf16[3584]{0:T(1024)(128)(2,1)} %g_hbm.3, bf16[256,3584]{1,0:T(8,128)(2,1)} %x_hbm.3, bf16[8192,128]{1,0:T(8,128)(2,1)} %bitcast.11, bf16[8192,128]{1,0:T(8,128)(2,1)} %bitcast.13, ...), custom_call_target="tpu_custom_call" | custom-call | tf_op jit(solution)/shard_map/layer/pallas_call | solution.py:409
  88.1 2.8 %copy.20 = bf16[256,3584]{1,0:T(8,128)(2,1)} copy(bf16[256,3584]{1,0:T(8,128)(2,1)} %layer.1) | data formatting | bytes 3670016

commit v6 on v5

--- a/solution.py
+++ b/solution.py
@@ -321,65 +321,66 @@
     chunk[...] = out
 
     cut = [(0, 2 * LANE), (2 * LANE, 2 * LANE), (4 * LANE, w - 4 * LANE)]
-    p1 = []
-    for p, (lo, n) in enumerate(cut):
-        for k, peer in enumerate(planes[p]):
-            src, dst = chunk.at[:, lo:lo + n], buf.at[z, y, c, x, :, lo:lo + n]
-            copy = remote(src, dst, p1_send.at[p, k], p1_recv.at[p, k], dev(*peer, c))
-            copy.start()
-            p1.append(copy)
+    order = (0, 1, 3, 2)
+    p1 = {}
+    for d in order:
+        for p, (lo, n) in enumerate(cut):
+            for k in range(15):
+                if XY[k][1] == d:
+                    src, dst = chunk.at[:, lo:lo + n], buf.at[z, y, c, x, :, lo:lo + n]
+                    p1[p, k] = remote(src, dst, p1_send.at[p, k], p1_recv.at[p, k], dev(*planes[p][k], c))
+                    p1[p, k].start()
     buf[z, y, c, x] = out
 
-    def block(p, v, h):
+    def line_of(p, v, d):
         lo, n = cut[p]
         cols_p = slice(lo, lo + n)
-        two = slice(2 * h, 2 * h + 2)
-        return [buf.at[v, two, c, :, :, cols_p], buf.at[two, :, c, v, :, cols_p], buf.at[two, v, c, :, :, cols_p]][p]
+        b = turn((y, y, z)[p], (4 - d) % 4, 4)
+        return [buf.at[v, b, c, :, :, cols_p], buf.at[:, b, c, v, :, cols_p], buf.at[b, v, c, :, :, cols_p]][p]
 
     here = [z, x, y]
     up1 = [dev(x, turn(z, 1, 4), y, c), dev(turn(x, 1, 4), z, y, c), dev(x, z, turn(y, 1, 4), c)]
     dn1 = [dev(x, turn(z, 3, 4), y, c), dev(turn(x, 3, 4), z, y, c), dev(x, z, turn(y, 3, 4), c)]
-    done = []
-
-    def send(p, v, h, to, i):
-        copy = remote(block(p, v, h), block(p, v, h), p2_send.at[p, i], p2_recv.at[p, i], to)
+    done, crossed = [], []
+
+    def send(p, v, d, to, kind):
+        ref = line_of(p, v, d)
+        copy = remote(ref, ref, p2_send.at[p, kind * 4 + d], p2_recv.at[p, kind * 4 + d], to)
         copy.start()
         done.append(copy)
         return copy
 
-    def across(p, v, h, i):
-        copy = remote(block(p, v, h), block(p, v, h), cc_send.at[p, i], cc_recv.at[p, i], partner)
+    def across(p, v, d, kind):
+        ref = line_of(p, v, d)
+        copy = remote(ref, ref, cc_send.at[p, kind * 4 + d], cc_recv.at[p, kind * 4 + d], partner)
         copy.start()
         done.append(copy)
-        return copy
-
-    direct, relayed, crossed = [], [], []
-    for p in range(3):
-        for copy in p1[p * 15:(p + 1) * 15]:
-            copy.wait_recv()
-        v = here[p]
-        direct.append([send(p, v, 0, up1[p], 0), send(p, v, 1, dn1[p], 1), send(p, v, 1, up1[p], 2), send(p, v, 0, dn1[p], 3)])
-        crossed += [across(p, v, 0, 0), across(p, v, 1, 1)]
-    for p in range(3):
-        below, above = turn(here[p], 3, 4), turn(here[p], 1, 4)
-        direct[p][0].wait_recv()
-        far = [send(p, below, 0, up1[p], 4)]
-        direct[p][1].wait_recv()
-        far += [send(p, above, 1, dn1[p], 5)]
-        relayed.append(far)
-        crossed += [across(p, below, 0, 2), across(p, above, 1, 3)]
-    for p in range(3):
-        below, above = turn(here[p], 3, 4), turn(here[p], 1, 4)
-        direct[p][2].wait_recv()
-        crossed += [across(p, below, 1, 4)]
-        direct[p][3].wait_recv()
-        crossed += [across(p, above, 0, 5)]
-    for p in range(3):
-        far = turn(here[p], 2, 4)
-        relayed[p][0].wait_recv()
-        crossed += [across(p, far, 0, 6)]
-        relayed[p][1].wait_recv()
-        crossed += [across(p, far, 1, 7)]
+        crossed.append(copy)
+
+    ups, downs, relays = {}, {}, {}
+    for d in order:
+        for p in range(3):
+            for k in range(15):
+                if XY[k][1] == d:
+                    p1[p, k].wait_recv()
+            ups[p, d] = send(p, here[p], d, up1[p], 0)
+            downs[p, d] = send(p, here[p], d, dn1[p], 1)
+            across(p, here[p], d, 0)
+    for d in order:
+        for p in range(3):
+            below, above = turn(here[p], 3, 4), turn(here[p], 1, 4)
+            ups[p, d].wait_recv()
+            if d < 2:
+                relays[p, d] = send(p, below, d, up1[p], 2)
+            downs[p, d].wait_recv()
+            if d >= 2:
+                relays[p, d] = send(p, above, d, dn1[p], 2)
+            across(p, below, d, 1)
+            across(p, above, d, 2)
+    for d in order:
+        for p in range(3):
+            relays[p, d].wait_recv()
+            across(p, turn(here[p], 2, 4), d, 3)
     for copy in crossed:
         copy.wait_recv()
     puts = []
@@ -393,7 +394,7 @@
         put = pltpu.make_async_copy(wd.at[at, :], out_hbm.at[at, :], out_sem.at[a])
         put.start()
         puts.append(put)
-    for copy in gives + [back] + rs + fw[1:] + xo + p1 + done:
+    for copy in gives + [back] + rs + fw[1:] + xo + list(p1.values()) + done:
         copy.wait_send()
     for put in puts:
         put.wait()
@@ -436,7 +437,7 @@
             sem((4, steps + 1)),
             sem((NZ,)),
             sem((6,)), sem((16,)), sem((16,)), sem((15,)), sem((15,)), sem((3,)), sem((3,)), sem((3,)), sem((3,)), sem((4,)), sem((4,)),
-            sem((2,)), sem((3,)), sem((3,)), sem((3, 15)), sem((3, 15)), sem((3, 6)), sem((3, 6)), sem((3, 8)), sem((3, 8)),
+            sem((2,)), sem((3,)), sem((3,)), sem((3, 15)), sem((3, 15)), sem((3, 12)), sem((3, 12)), sem((3, 16)), sem((3, 16)),
         ],
         compiler_params=pltpu.CompilerParams(collective_id=0, has_side_effects=True, vmem_limit_bytes=VMEM_ALL),
     )(q, pos, g, x_tok, ko.reshape(keys, LANE), vo.reshape(keys, LANE), wo, wg, wu, wd)
@@ -445,10 +446,7 @@
 GRP = 16
 
 
-def project_kernel(
-    lens_hbm, line_hbm, g_hbm, freq_hbm, x_hbm, k_hbm, v_hbm, wq_hbm, wk_hbm, wv_hbm, q_hbm, pos_hbm, ko_hbm, vo_hbm,
-    lens_ref, lens_row, g_ref, freq_ref, q_ref, pos_ref, xs, u, w, kv, knew, vnew, sem, small_sem, out_sem, q_sem,
-):
+def project_kernel(lens_ref, lens_row, g_ref, freq_ref, x_hbm, k_hbm, v_hbm, wq_hbm, wk_hbm, wv_hbm, q_ref, pos_ref, ko_hbm, vo_hbm, xs, u, w, kv, knew, vnew, sem, out_sem):
     rows, width = xs.shape
     heads = q_ref.shape[0]
     hd = heads * LANE
@@ -465,16 +463,8 @@
     get_cache = [pltpu.make_async_copy(k_hbm, kv.at[0], sem.at[4]), pltpu.make_async_copy(v_hbm, kv.at[1], sem.at[5])]
     cuts = [(i, min(2 * LANE, hd - i)) for i in range(0, hd, 2 * LANE)]
     get_q = [pltpu.make_async_copy(wq_hbm.at[:, i:i + n], w.at[:, i:i + n], sem.at[6 + j]) for j, (i, n) in enumerate(cuts)]
-    get_small = [
-        pltpu.make_async_copy(line_hbm, lens_row, small_sem.at[0]),
-        pltpu.make_async_copy(freq_hbm, freq_ref, small_sem.at[1]),
-        pltpu.make_async_copy(g_hbm, g_ref, small_sem.at[2]),
-        pltpu.make_async_copy(lens_hbm, lens_ref, small_sem.at[3]),
-    ]
-    for copy in get_small + get_x + get_kv + get_cache + get_q:
-        copy.start()
-    for copy in get_small[:3]:
-        copy.wait()
+    for copy in get_x + get_kv + get_cache + get_q:
+        copy.start()
 
     eye = lax.broadcasted_iota(jnp.int32, (LANE, LANE), 0) == lax.broadcasted_iota(jnp.int32, (LANE, LANE), 1)
     cols = []
@@ -483,8 +473,6 @@
         col = jnp.sum(jnp.where(eye, line, 0.0), axis=1, keepdims=True)
         pos_ref[i * LANE:(i + 1) * LANE, :] = jnp.broadcast_to(col, (LANE, LANE)).astype(jnp.int32)
         cols.append(col)
-    puts = [pltpu.make_async_copy(pos_ref, pos_hbm, q_sem.at[len(cuts)])]
-    puts[0].start()
     low = lax.broadcasted_iota(jnp.int32, (LANE, LANE), 1) < half
     angles = jnp.where(low, cols[0], cols[1]) * freq_ref[...]
     cos = jnp.cos(angles)
@@ -513,7 +501,7 @@
     out = jnp.dot(u[...], w[:, hd:], preferred_element_type=F32).astype(BF16).astype(F32)
     knew[...] = rope(out[:, :LANE]).astype(F32)
     vnew[...] = out[:, LANE:]
-    for copy in get_cache + get_small[3:]:
+    for copy in get_cache:
         copy.wait()
     line = lax.broadcasted_iota(jnp.int32, (seq, LANE), 0)
 
@@ -525,6 +513,7 @@
             kv[1, b] = jnp.where(here, vnew[pl.ds(b, 1), :], kv[1, b].astype(F32)).astype(BF16)
         return carry
 
+    puts = []
     part = rows // n_out
     for i in range(n_out):
         lax.fori_loop(i * part // GRP, (i + 1) * part // GRP, put, 0)
@@ -533,15 +522,11 @@
             copy = pltpu.make_async_copy(kv.at[j, at], ref.at[at], out_sem.at[j, i])
             copy.start()
             puts.append(copy)
-    for i, (copy, (a, n)) in enumerate(zip(get_q, cuts)):
+    for copy, (a, n) in zip(get_q, cuts):
         copy.wait()
         out = jnp.dot(u[...], w[:, a:a + n], preferred_element_type=F32).astype(BF16).astype(F32)
         for j in range(0, n, LANE):
             q_ref[(a + j) // LANE] = rope(out[:, j:j + LANE])
-        at = slice(a // LANE, (a + n) // LANE)
-        copy = pltpu.make_async_copy(q_ref.at[at], q_hbm.at[at], q_sem.at[i])
-        copy.start()
-        puts.append(copy)
     for copy in puts:
         copy.wait()
 
@@ -553,6 +538,7 @@
     half = LANE // 2
     freq = np.float32(ROPE_BASE) ** (np.arange(half, dtype=np.float32) * np.float32(-2.0 / LANE))
     freq = jnp.asarray(np.concatenate([freq, freq]).reshape(1, LANE).astype(np.float32))
+    vmem = pl.BlockSpec(memory_space=pltpu.VMEM)
     hbm = pl.BlockSpec(memory_space=pl.ANY)
     sem = pltpu.SemaphoreType.DMA
     cache = jax.ShapeDtypeStruct((rows, seq, LANE), BF16)
@@ -565,15 +551,9 @@
             cache,
             cache,
         ],
-        in_specs=[hbm] * 10,
-        out_specs=[hbm] * 4,
+        in_specs=[pl.BlockSpec(memory_space=pltpu.SMEM), vmem, vmem, vmem] + [hbm] * 6,
+        out_specs=[vmem, vmem, hbm, hbm],
         scratch_shapes=[
-            pltpu.SMEM(seq_lens.shape, jnp.int32),
-            pltpu.VMEM((rows // LANE, LANE), jnp.int32),
-            pltpu.VMEM(g.shape, BF16),
-            pltpu.VMEM((1, LANE), F32),
-            pltpu.VMEM((hd // LANE, rows, LANE), BF16),
-            pltpu.VMEM((rows, LANE), jnp.int32),
             pltpu.VMEM((rows, width), BF16),
             pltpu.VMEM((rows, width), BF16),
             pltpu.VMEM((width, hd + 2 * LANE), BF16),
@@ -581,9 +561,7 @@
             pltpu.VMEM((rows, LANE), F32),
             pltpu.VMEM((rows, LANE), F32),
             sem((10,)),
-            sem((4,)),
             sem((2, 4)),
-            sem((6,)),
         ],
         compiler_params=pltpu.CompilerParams(vmem_limit_bytes=VMEM_ALL),
     )(seq_lens, seq_lens.reshape(rows // LANE, LANE), g, freq, x_tok, k_blk.reshape(cache.shape), v_blk.reshape(cache.shape), wq, wk, wv)

time: 91.1 us -> 87.7 us (0.963)
  Pallas kernels: 87.5 us -> 84.1 us
    pallas_call x1, Pallas kernels: 14.2 us -> 11.6 us  [project(): pl.pallas_call(project_kernel, name='project', out_shape=[jax.ShapeDtypeS...]
where the time goes in v6:
time: 87.7 us; the launch traced here: 87.6 us
  Pallas kernels  84.1 us (96%)
  local copies, waits for them, and re-layouts  2.85 us (3%)
    pallas_call x1, Pallas kernels, layer(): pl.pallas_call(layer_kernel, name='layer', out_shape=jax.ShapeDtypeStruct...  72.5 us
    pallas_call x1, Pallas kernels, project(): pl.pallas_call(project_kernel, name='project', out_shape=[jax.ShapeDtypeS...  11.6 us
    unnamed x1, local copies, waits for them, and re-layouts  2.85 us

profile of v6, /device:TPU:1, one launch (start us, length us, event | category | flops | bytes accessed | tf_op | source)
XLA Modules:
  0.0 87.6 jit_solution(8184715044558445441)
XLA Ops:
  0.6 11.6 %project.1 = (bf16[7,256,128]{2,1,0:T(8,128)(2,1)}, s32[256,128]{1,0:T(8,128)}, bf16[256,32,128]{2,1,0:T(8,128)(2,1)}, bf16[256,32,128]{2,1,0:T(8,128)(2,1)}) custom-call(s32[256]{0:T(256)} %lens_ref.1, s32[2,128]{1,0:T(2,128)} %bitcast.17, bf16[3584]{0:T(1024)(128)(2,1)} %g_ref.1, f32[1,128]{1,0:T(1,128)} %constant.2.clone.freq_ref, ...), custom_call_target="tpu_custom_call" | custom-call | tf_op jit(solution)/shard_map/project/pallas_call | solution.py:545
  12.2 72.5 %layer.1 = bf16[256,3584]{1,0:T(8,128)(2,1)} custom-call(bf16[7,256,128]{2,1,0:T(8,128)(2,1)} %get-tuple-element.7.q_hbm, s32[256,128]{1,0:T(8,128)} %get-tuple-element.8.pos_hbm, bf16[3584]{0:T(1024)(128)(2,1)} %g_hbm.1, bf16[256,3584]{1,0:T(8,128)(2,1)} %x_hbm.3, bf16[8192,128]{1,0:T(8,128)(2,1)} %bitcast.11, bf16[8192,128]{1,0:T(8,128)(2,1)} %bitcast.13, ...), custom_call_target="tpu_custom_call" | custom-call | tf_op jit(solution)/shard_map/layer/pallas_call | solution.py:410
  84.7 2.8 %copy.20 = bf16[256,3584]{1,0:T(8,128)(2,1)} copy(bf16[256,3584]{1,0:T(8,128)(2,1)} %layer.1) | data formatting | bytes 3670016

commit v7 on v6

--- a/solution.py
+++ b/solution.py
@@ -48,10 +48,10 @@
 
 def layer_kernel(
     q_hbm, pos_hbm, g_hbm, x_hbm, k_hbm, v_hbm, wo_hbm, wg_hbm, wu_hbm, wd_hbm, out_hbm,
-    q_ref, pos_ref, g_ref, kv, res, pack, swap, merged, slots, part, xslots, chunk, hid, hn, acc, cslot, buf,
+    q_ref, pos_ref, g_ref, kv, res, pack, swap, merged, slots, part, xslots, chunk, hid, hn, acts, acc, outs, cslot, buf,
     wg, wu, wd,
     w_sem, out_sem, in_sem, gv_send, gv_recv, rs_send, rs_recv, xs_send, xs_recv, ag_send, ag_recv, fw_send, fw_recv,
-    c_sem, xo_send, xo_recv, p1_send, p1_recv, p2_send, p2_recv, cc_send, cc_recv,
+    c_send, c_recv, xo_send, xo_recv, p1_send, p1_recv, p2_send, p2_recv, cc_send, cc_recv,
 ):
     x, z, y, c = coords()
     w = chunk.shape[1]
@@ -99,7 +99,6 @@
     ]
     for copy in (get_in[3], get_in[4], get_in[0], get_in[1], get_in[2], get_in[5]):
         copy.start()
-    fetch(0)[0].start()
     planes = [
         [(turn(x, a, NX), z, turn(y, b, NY)) for a, b in XY],
         [(x, turn(z, a, NZ), turn(y, b, NY)) for a, b in XY],
@@ -174,6 +173,8 @@
     lag = 4
     for i in (0, 1, 3, 4):
         get_in[i].wait()
+    get_wo.start()
+    fetch(0)[0].start()
 
     def begin(k, carry):
         attend(k)
@@ -196,7 +197,6 @@
     rs = [deliver(k) for k in range(n_grp - 1)]
     gives = [give(k) for k in range(n_grp)]
     early = 1 + (n_grp - lag) // 2
-    get_wo.start()
     for i in range(steps):
         fetch(i)[1].start()
     for i in range(early, steps):
@@ -267,7 +267,6 @@
     h32 = hid[...]
     inv = lax.rsqrt(jnp.mean(h32 * h32, axis=-1, keepdims=True) + NORM_EPS)
     hn[...] = (h32 * inv * g_ref[...].astype(F32)).astype(BF16)
-    acc[...] = jnp.zeros_like(acc)
     mid = (ff // LANE + 1) // 2 * LANE
 
     def gated(gate, up, start):
@@ -285,9 +284,7 @@
         cu.wait()
         up = jnp.dot(hn[...], wu[i], preferred_element_type=F32)
         act = gated(gate, up, first + i * WIN)
-        fetch_down(i).wait()
-        here = pl.ds(pl.multiple_of(i * WIN, LANE), WIN)
-        acc[...] += jnp.dot(act, wd[here, :], preferred_element_type=F32)
+        acts[:, pl.ds(pl.multiple_of(i * WIN, LANE), WIN)] = act
         return carry
 
     lax.fori_loop(0, steps, mlp_step, 0)
@@ -295,23 +292,36 @@
     gate = jnp.dot(hn[...], wg_t[...], preferred_element_type=F32)
     tails[1].wait()
     up = jnp.dot(hn[...], wu_t[...], preferred_element_type=F32)
-    act = gated(gate, up, first + wide)
+    acts[:, wide:] = gated(gate, up, first + wide)
+    for i in range(steps):
+        fetch_down(i).wait()
     tails[2].wait()
-    acc[...] += jnp.dot(act, wd[wide:, :], preferred_element_type=F32)
 
     mate_rows = pl.ds(pl.multiple_of(mate * 8, 8), 8)
-    back = remote(acc.at[mate_rows, :], cslot, c_sem.at[0], c_sem.at[1], partner)
-    back.start()
+    hops = (2, 1, 3, 0)
+    back, xo = [], []
+
+    def to_owner(j):
+        back[j].wait_recv()
+        outs[j] = acc[j, my_rows, :] + cslot[j]
+        owner = dev(turn(x, hops[j], NX), z, y, c)
+        copy = remote(outs.at[j], xslots.at[j + 3], xo_send.at[j], xo_recv.at[j], owner)
+        copy.start()
+        xo.append(copy)
+
+    for j, hop in enumerate(hops):
+        own = pl.ds(pl.multiple_of(turn(x, hop, NX) * w, LANE), w)
+        acc[j] = jnp.dot(acts[...], wd[:, own], preferred_element_type=F32)
+        copy = remote(acc.at[j, mate_rows, :], cslot.at[j], c_send.at[j], c_recv.at[j], partner)
+        copy.start()
+        back.append(copy)
+        if j >= 2:
+            to_owner(j - 2)
+    to_owner(2)
+    back[3].wait_recv()
+    sums = acc[3, my_rows, :] + cslot[3]
     for copy in xs:
         copy.wait_send()
-    back.wait_recv()
-    part[...] = acc[my_rows, :] + cslot[...]
-    xo = []
-    for k, px in enumerate(line):
-        copy = remote(part.at[:, cols[k]], xslots.at[k + 3], xo_send.at[k], xo_recv.at[k], dev(px, z, y, c))
-        copy.start()
-        xo.append(copy)
-    sums = part[:, my_cols]
     for k, copy in enumerate(xo):
         copy.wait_recv()
         sums = sums + xslots[k + 3]
@@ -341,6 +351,7 @@
     here = [z, x, y]
     up1 = [dev(x, turn(z, 1, 4), y, c), dev(turn(x, 1, 4), z, y, c), dev(x, z, turn(y, 1, 4), c)]
     dn1 = [dev(x, turn(z, 3, 4), y, c), dev(turn(x, 3, 4), z, y, c), dev(x, z, turn(y, 3, 4), c)]
+    far1 = [dev(x, turn(z, 2, 4), y, c), dev(turn(x, 2, 4), z, y, c), dev(x, z, turn(y, 2, 4), c)]
     done, crossed = [], []
 
     def send(p, v, d, to, kind):
@@ -365,6 +376,8 @@
                     p1[p, k].wait_recv()
             ups[p, d] = send(p, here[p], d, up1[p], 0)
             downs[p, d] = send(p, here[p], d, dn1[p], 1)
+            if d == 2:
+                relays[p, d] = send(p, here[p], d, far1[p], 2)
             across(p, here[p], d, 0)
     for d in order:
         for p in range(3):
@@ -373,7 +386,7 @@
             if d < 2:
                 relays[p, d] = send(p, below, d, up1[p], 2)
             downs[p, d].wait_recv()
-            if d >= 2:
+            if d == 3:
                 relays[p, d] = send(p, above, d, dn1[p], 2)
             across(p, below, d, 1)
             across(p, above, d, 2)
@@ -394,7 +407,7 @@
         put = pltpu.make_async_copy(wd.at[at, :], out_hbm.at[at, :], out_sem.at[a])
         put.start()
         puts.append(put)
-    for copy in gives + [back] + rs + fw[1:] + xo + list(p1.values()) + done:
+    for copy in gives + back + rs + fw[1:] + xo + list(p1.values()) + done:
         copy.wait_send()
     for put in puts:
         put.wait()
@@ -428,8 +441,10 @@
             pltpu.VMEM((8, w), F32),
             pltpu.VMEM((8 * NC, width), F32),
             pltpu.VMEM((8 * NC, width), BF16),
-            pltpu.VMEM((8 * NC, width), F32),
-            pltpu.VMEM((8, width), F32),
+            pltpu.VMEM((8 * NC, steps * WIN + LANE), BF16),
+            pltpu.VMEM((NX, 8 * NC, w), F32),
+            pltpu.VMEM((NX - 1, 8, w), F32),
+            pltpu.VMEM((NX, 8, w), F32),
             pltpu.VMEM((NZ, NY, NC, NX, 8, w), F32),
             pltpu.VMEM((steps, width, WIN), BF16),
             pltpu.VMEM((steps, width, WIN), BF16),
@@ -437,7 +452,7 @@
             sem((4, steps + 1)),
             sem((NZ,)),
             sem((6,)), sem((16,)), sem((16,)), sem((15,)), sem((15,)), sem((3,)), sem((3,)), sem((3,)), sem((3,)), sem((4,)), sem((4,)),
-            sem((2,)), sem((3,)), sem((3,)), sem((3, 15)), sem((3, 15)), sem((3, 12)), sem((3, 12)), sem((3, 16)), sem((3, 16)),
+            sem((4,)), sem((4,)), sem((3,)), sem((3,)), sem((3, 15)), sem((3, 15)), sem((3, 12)), sem((3, 12)), sem((3, 16)), sem((3, 16)),
         ],
         compiler_params=pltpu.CompilerParams(collective_id=0, has_side_effects=True, vmem_limit_bytes=VMEM_ALL),
     )(q, pos, g, x_tok, ko.reshape(keys, LANE), vo.reshape(keys, LANE), wo, wg, wu, wd)
@@ -463,8 +478,9 @@
     get_cache = [pltpu.make_async_copy(k_hbm, kv.at[0], sem.at[4]), pltpu.make_async_copy(v_hbm, kv.at[1], sem.at[5])]
     cuts = [(i, min(2 * LANE, hd - i)) for i in range(0, hd, 2 * LANE)]
     get_q = [pltpu.make_async_copy(wq_hbm.at[:, i:i + n], w.at[:, i:i + n], sem.at[6 + j]) for j, (i, n) in enumerate(cuts)]
-    for copy in get_x + get_kv + get_cache + get_q:
-        copy.start()
+    for copy in get_x:
+        copy.start()
+    then = [get_kv + get_cache, get_q]
 
     eye = lax.broadcasted_iota(jnp.int32, (LANE, LANE), 0) == lax.broadcasted_iota(jnp.int32, (LANE, LANE), 1)
     cols = []
@@ -491,6 +507,8 @@
 
     for i in range(n_x):
         get_x[i].wait()
+        for copy in then[i]:
+            copy.start()
         lax.fori_loop(i * part // GRP, (i + 1) * part // GRP, norm, 0)
 
     def rope(t):

time: 87.7 us -> 85.9 us (0.979)
  Pallas kernels: 84.1 us -> 82.2 us
    pallas_call x1, Pallas kernels: 72.5 us -> 70.6 us  [layer(): pl.pallas_call(layer_kernel, name='layer', out_shape=jax.ShapeDtypeStruct...]
where the time goes in v7:
time: 85.9 us; the launch traced here: 85.7 us
  Pallas kernels  82.2 us (96%)
  local copies, waits for them, and re-layouts  2.85 us (3%)
    pallas_call x1, Pallas kernels, layer(): pl.pallas_call(layer_kernel, name='layer', out_shape=jax.ShapeDtypeStruct...  70.6 us
    pallas_call x1, Pallas kernels, project(): pl.pallas_call(project_kernel, name='project', out_shape=[jax.ShapeDtypeS...  11.6 us
    unnamed x1, local copies, waits for them, and re-layouts  2.85 us

profile of v7, /device:TPU:1, one launch (start us, length us, event | category | flops | bytes accessed | tf_op | source)
XLA Modules:
  0.0 85.7 jit_solution(14484665695818085350)
XLA Ops:
  0.6 11.6 %project.1 = (bf16[7,256,128]{2,1,0:T(8,128)(2,1)}, s32[256,128]{1,0:T(8,128)}, bf16[256,32,128]{2,1,0:T(8,128)(2,1)}, bf16[256,32,128]{2,1,0:T(8,128)(2,1)}) custom-call(s32[256]{0:T(256)} %lens_ref.1, s32[2,128]{1,0:T(2,128)} %bitcast.17, bf16[3584]{0:T(1024)(128)(2,1)} %g_ref.1, f32[1,128]{1,0:T(1,128)} %constant.2.clone.freq_ref, ...), custom_call_target="tpu_custom_call" | custom-call | tf_op jit(solution)/shard_map/project/pallas_call | solution.py:563
  12.2 70.6 %layer.1 = bf16[256,3584]{1,0:T(8,128)(2,1)} custom-call(bf16[7,256,128]{2,1,0:T(8,128)(2,1)} %get-tuple-element.7.q_hbm, s32[256,128]{1,0:T(8,128)} %get-tuple-element.8.pos_hbm, bf16[3584]{0:T(1024)(128)(2,1)} %g_hbm.1, bf16[256,3584]{1,0:T(8,128)(2,1)} %x_hbm.3, bf16[8192,128]{1,0:T(8,128)(2,1)} %bitcast.11, bf16[8192,128]{1,0:T(8,128)(2,1)} %bitcast.13, ...), custom_call_target="tpu_custom_call" | custom-call | tf_op jit(solution)/shard_map/layer/pallas_call | solution.py:423
  82.9 2.8 %copy.20 = bf16[256,3584]{1,0:T(8,128)(2,1)} copy(bf16[256,3584]{1,0:T(8,128)(2,1)} %layer.1) | data formatting | bytes 3670016

commit v8 on v7

--- a/solution.py
+++ b/solution.py
@@ -113,8 +113,11 @@
     span = GRP * seq
     low = lax.broadcasted_iota(jnp.int32, (8, LANE), 1) < half
 
+    def far_first(i):
+        return (2 + i + i // 2 + 2 * (i // 3)) % 4
+
     def place(k):
-        return turn(z, ((k + 1) // NY) % NZ, NZ), turn(y, (k + 1) % NY, NY)
+        return turn(z, far_first(k // NY), NZ), turn(y, far_first(k % NY), NY)
 
     def give(k):
         return remote(pack.at[k, mate], swap.at[k], gv_send.at[k], gv_recv.at[k], partner)
@@ -221,31 +224,34 @@
     attn = jnp.concatenate([mixed[h] / total[:, half + h:half + h + 1] for h in range(heads)], axis=1).astype(BF16)
 
     get_wo.wait()
-    for n in range(0, part.shape[1], 4 * LANE):
-        part[:, n:n + 4 * LANE] = jnp.dot(attn, wd[keep:, n:n + 4 * LANE], preferred_element_type=F32)
     my_cols = pl.ds(pl.multiple_of(x * w, LANE), w)
     my_rows = pl.ds(pl.multiple_of(c * 8, 8), 8)
     line = [turn(x, k, NX) for k in range(1, NX)]
     cols = [pl.ds(pl.multiple_of(px * w, LANE), w) for px in line]
+    hops = (2, 1, 3, 0)
     xs = []
-    for k, px in enumerate(line):
-        copy = remote(part.at[:, cols[k]], xslots.at[k], xs_send.at[k], xs_recv.at[k], dev(px, z, y, c))
-        copy.start()
-        xs.append(copy)
+    for j, hop in enumerate(hops):
+        px = turn(x, hop, NX)
+        own = pl.ds(pl.multiple_of(px * w, LANE), w)
+        here = slice(j * w, (j + 1) * w)
+        part[:, here] = jnp.dot(attn, wd[keep:, own], preferred_element_type=F32)
+        if hop:
+            copy = remote(part.at[:, here], xslots.at[j], xs_send.at[j], xs_recv.at[j], dev(px, z, y, c))
+            copy.start()
+            xs.append(copy)
     for i in range(1, 5):
         fetch_down(i).start()
-    sums = part[:, my_cols]
+    sums = part[:, 3 * w:]
     for k, copy in enumerate(xs):
         copy.wait_recv()
         sums = sums + xslots[k]
     get_in[2].wait()
     hidden = (res[...].astype(F32) + sums).astype(BF16).astype(F32)
     chunk[...] = hidden
-    ag = []
-    for k, px in enumerate(line):
-        copy = remote(chunk, hid.at[my_rows, my_cols], ag_send.at[k], ag_recv.at[k], dev(px, z, y, c))
-        copy.start()
-        ag.append(copy)
+    ag = [None] * 3
+    for k in (1, 0, 2):
+        ag[k] = remote(chunk, hid.at[my_rows, my_cols], ag_send.at[k], ag_recv.at[k], dev(line[k], z, y, c))
+        ag[k].start()
     fw = [remote(chunk, hid.at[my_rows, my_cols], fw_send.at[3], fw_recv.at[3], partner)]
     fw[0].start()
     hid[my_rows, my_cols] = hidden
@@ -253,8 +259,8 @@
         fetch_down(i).start()
     for copy in tails:
         copy.start()
-    for k, copy in enumerate(ag):
-        copy.wait_recv()
+    for k in (0, 2, 1):
+        ag[k].wait_recv()
         block = hid.at[my_rows, cols[2 - k]]
         copy = remote(block, block, fw_send.at[k], fw_recv.at[k], partner)
         copy.start()
@@ -298,7 +304,6 @@
     tails[2].wait()
 
     mate_rows = pl.ds(pl.multiple_of(mate * 8, 8), 8)
-    hops = (2, 1, 3, 0)
     back, xo = [], []
 
     def to_owner(j):

time: 85.9 us -> 84.4 us (0.983)
  Pallas kernels: 82.2 us -> 80.7 us
    pallas_call x1, Pallas kernels: 70.6 us -> 69.1 us  [layer(): pl.pallas_call(layer_kernel, name='layer', out_shape=jax.ShapeDtypeStruct...]
where the time goes in v8:
time: 84.4 us; the launch traced here: 84.2 us
  Pallas kernels  80.7 us (96%)
  local copies, waits for them, and re-layouts  2.85 us (3%)
    pallas_call x1, Pallas kernels, layer(): pl.pallas_call(layer_kernel, name='layer', out_shape=jax.ShapeDtypeStruct...  69.1 us
    pallas_call x1, Pallas kernels, project(): pl.pallas_call(project_kernel, name='project', out_shape=[jax.ShapeDtypeS...  11.6 us
    unnamed x1, local copies, waits for them, and re-layouts  2.85 us

profile of v8, /device:TPU:1, one launch (start us, length us, event | category | flops | bytes accessed | tf_op | source)
XLA Modules:
  0.0 84.2 jit_solution(13538046149540314747)
XLA Ops:
  0.6 11.6 %project.1 = (bf16[7,256,128]{2,1,0:T(8,128)(2,1)}, s32[256,128]{1,0:T(8,128)}, bf16[256,32,128]{2,1,0:T(8,128)(2,1)}, bf16[256,32,128]{2,1,0:T(8,128)(2,1)}) custom-call(s32[256]{0:T(256)} %lens_ref.1, s32[2,128]{1,0:T(2,128)} %bitcast.17, bf16[3584]{0:T(1024)(128)(2,1)} %g_ref.1, f32[1,128]{1,0:T(1,128)} %constant.2.clone.freq_ref, ...), custom_call_target="tpu_custom_call" | custom-call | tf_op jit(solution)/shard_map/project/pallas_call | solution.py:568
  12.2 69.1 %layer.1 = bf16[256,3584]{1,0:T(8,128)(2,1)} custom-call(bf16[7,256,128]{2,1,0:T(8,128)(2,1)} %get-tuple-element.7.q_hbm, s32[256,128]{1,0:T(8,128)} %get-tuple-element.8.pos_hbm, bf16[3584]{0:T(1024)(128)(2,1)} %g_hbm.1, bf16[256,3584]{1,0:T(8,128)(2,1)} %x_hbm.3, bf16[8192,128]{1,0:T(8,128)(2,1)} %bitcast.11, bf16[8192,128]{1,0:T(8,128)(2,1)} %bitcast.13, ...), custom_call_target="tpu_custom_call" | custom-call | tf_op jit(solution)/shard_map/layer/pallas_call | solution.py:428
  81.3 2.8 %copy.20 = bf16[256,3584]{1,0:T(8,128)(2,1)} copy(bf16[256,3584]{1,0:T(8,128)(2,1)} %layer.1) | data formatting | bytes 3670016
